TPU v7x, 32 devices: a whole 2x2x4 slice. The times are simulated.
32 devices in a mesh: sp: 2 (over core), py: 4 (over z), pz: 4 (over y, x).
Axes of the slice: x: 2, y: 2, z: 4, core: 2. Of those that a mesh axis runs over, the one named last changes fastest.
Arguments:
- concentration: float32 [8, 128, 128, 128], P('sp', 'py', 'pz'), may hold values from -1 to 1.1
- mobility: float32 [8, 8], replicated, may hold values from 0.1 to 0.6
- kappa: float32 [8], replicated, may hold values from 0.5 to 2
- well_depth: float32 [8], P('sp'), may hold values from 0.5 to 2
Outputs:
- updated: float32 [8, 128, 128, 128], P('sp', 'py', 'pz')
All inputs are finite; a program needn't handle non-finite values.
Results may differ from a plain program's by a relative error of at most 0.000084.
Values sent between devices are 32-bit elements; how exact they have to be, the bound alone decides.
A program may use at most 128 MiB of HBM per device.

v0:
```python
import functools
import math

import jax
import jax.numpy as jnp
import numpy as np
from jax import lax
from jax.experimental import pallas as pl
from jax.experimental.pallas import tpu as pltpu
from jax.sharding import PartitionSpec as P


def tables(count):
    modes = jnp.arange(count, dtype=jnp.int32)
    product = modes[:, None] * modes[None, :] % count
    angle = 2.0 * math.pi * product.astype(jnp.float32) / count
    return (jnp.cos(angle), jnp.sin(angle))


def wave_square(index, count):
    freq = jnp.where(index < count // 2, index, index - count).astype(jnp.float32)
    return (2.0 * math.pi * freq / count) ** 2


def contract(form, values, table):
    return jnp.einsum(form, values, table, precision=lax.Precision.HIGHEST)


def rotate(spectrum, form, count, forward):
    cosine, sine = tables(count)
    real_part, imag_part = (spectrum[0], spectrum[1])
    real_cos = contract(form, real_part, cosine)
    real_sin = contract(form, real_part, sine)
    imag_cos = contract(form, imag_part, cosine)
    imag_sin = contract(form, imag_part, sine)
    if forward:
        return jnp.stack([real_cos + imag_sin, imag_cos - real_sin])
    return jnp.stack([real_cos - imag_sin, imag_cos + real_sin])


def per_device_general(concentration, mobility, kappa, well_depth):
    local_species, rows_x, rows_y, depth = concentration.shape
    count_sp = lax.axis_size("sp")
    count_py = lax.axis_size("py")
    count_pz = lax.axis_size("pz")
    full_x = rows_x * count_py
    full_y = rows_y * count_pz
    half_depth = depth // 2
    bulk = well_depth[:, None, None, None] * (
        concentration * concentration * concentration - concentration
    )
    fields = jnp.stack([concentration, bulk])
    cosine, sine = tables(depth)
    alternate = (1 - 2 * (jnp.arange(depth, dtype=jnp.int32) % 2)).astype(jnp.float32)
    spectrum = jnp.stack(
        [
            contract("fsxyz,zk->fsxyk", fields, cosine[:, :half_depth]),
            -contract("fsxyz,zk->fsxyk", fields, sine[:, :half_depth]),
        ]
    )
    spectrum = lax.all_to_all(spectrum, "pz", split_axis=5, concat_axis=4, tiled=True)
    own_lines = spectrum.shape[5]
    highest = contract("fsxyz,z->fsxy", fields, alternate)
    highest = lax.all_gather(highest, "pz", axis=3, tiled=True)
    highest = jnp.stack([highest, jnp.zeros_like(highest)])[..., None]
    spectrum = jnp.concatenate([spectrum, highest], axis=5)
    z_modes = jnp.concatenate(
        [
            lax.axis_index("pz") * own_lines + jnp.arange(own_lines, dtype=jnp.int32),
            jnp.full((1,), half_depth, jnp.int32),
        ]
    )
    spectrum = rotate(spectrum, "fsxyz,yk->fsxkz", full_y, True)
    spectrum = lax.all_to_all(
        lax.all_to_all(spectrum, "sp", split_axis=4, concat_axis=2, tiled=True),
        "py",
        split_axis=4,
        concat_axis=3,
        tiled=True,
    )
    spectrum = rotate(spectrum, "fsxyz,xk->fskyz", full_x, True)
    narrow = spectrum.shape[4]
    lines = spectrum.shape[5]
    y_start = (lax.axis_index("sp") * count_py + lax.axis_index("py")) * narrow
    ksq_x = wave_square(jnp.arange(full_x, dtype=jnp.int32), full_x)
    ksq_y = wave_square(y_start + jnp.arange(narrow, dtype=jnp.int32), full_y)
    ksq_z = wave_square(z_modes, depth)
    ksq = ksq_x[:, None, None] + ksq_y[None, :, None] + ksq_z[None, None, :]
    c_hat = spectrum[:, 0]
    drive = spectrum[:, 1] + kappa[None, :, None, None, None] * ksq[None, None] * c_hat
    mix = jnp.einsum("ij,rjxyz->rixyz", mobility, drive, precision=lax.Precision.HIGHEST)
    stiff = 0.5 * (jnp.diagonal(mobility) * kappa)[:, None, None, None] * (ksq * ksq)[None]
    new_hat = (c_hat * (1.0 + stiff)[None] - 0.5 * ksq[None, None] * mix) / (1.0 + stiff)[None]
    new_hat = rotate(new_hat, "sxyz,xk->skyz", full_x, False)
    moved = lax.all_to_all(
        lax.all_to_all(new_hat, "sp", split_axis=1, concat_axis=3, tiled=True),
        "py",
        split_axis=2,
        concat_axis=3,
        tiled=True,
    )
    moved = moved.reshape(2, local_species, rows_x, count_py, count_sp, narrow, lines)
    moved = moved.transpose(0, 1, 2, 4, 3, 5, 6).reshape(2, local_species, rows_x, full_y, lines)
    moved = rotate(moved, "sxyz,yk->sxkz", full_y, False)
    main = moved[..., : lines - 1]
    highest = moved[0, :, :, :, lines - 1]
    main = lax.all_to_all(main, "pz", split_axis=3, concat_axis=4, tiled=True)
    highest = lax.dynamic_slice_in_dim(highest, lax.axis_index("pz") * rows_y, rows_y, 2)
    weight = jnp.where(jnp.arange(half_depth, dtype=jnp.int32) == 0, 1.0, 2.0).astype(jnp.float32)
    result = contract("sxyk,kz->sxyz", main[0] * weight, cosine[:half_depth]) - contract(
        "sxyk,kz->sxyz", main[1] * weight, sine[:half_depth]
    )
    result = result + highest[..., None] * alternate[None, None, None, :]
    return result * (1.0 / (full_x * full_y * depth))


PIECES = 4
SUBLANES = 8


def basis(count):
    grid = np.arange(count)
    mode = np.arange(count)
    freq = np.minimum(mode, count - mode)
    angle = 2.0 * np.pi * (grid[:, None] * freq[None, :] % count) / count
    table = np.where(mode[None, :] <= count // 2, np.cos(angle), np.sin(angle))
    single = (mode == 0) | (2 * mode == count)
    return table * np.sqrt(np.where(single, 1.0, 2.0) / count)[None, :]


def split_table(table):
    table = table.astype(np.float32)
    high = table.astype(jnp.bfloat16)
    low = (table - high.astype(np.float32)).astype(jnp.bfloat16)
    row = np.concatenate([high, low], axis=1)
    return np.concatenate([row, row], axis=0)


def split(values, axis):
    high = values.astype(jnp.bfloat16)
    low = (values - high.astype(jnp.float32)).astype(jnp.bfloat16)
    return jnp.concatenate([high, low], axis=axis)


def from_right(values, table):
    count = values.shape[1]
    out = jnp.dot(split(values, 1), table, preferred_element_type=jnp.float32)
    return out[:, :count] + out[:, count:]


def from_left(table, values):
    count = table.shape[0] // 2
    out = jnp.dot(table, split(values, 0), preferred_element_type=jnp.float32)
    return out[:count] + out[count:]


def swap_blocks(parts, width):
    parts = list(parts)
    axis = parts[0].ndim - 1
    lanes = parts[0].shape[axis]
    block = lax.broadcasted_iota(jnp.int32, parts[0].shape, axis) // width
    half = len(parts) // 2
    while half:
        low_side = (block // half) % 2 == 0
        for first in range(len(parts)):
            if (first // half) % 2 == 0:
                one, two = parts[first], parts[first + half]
                parts[first] = jnp.where(low_side, one, pltpu.roll(two, half * width, axis))
                parts[first + half] = jnp.where(
                    low_side, pltpu.roll(one, lanes - half * width, axis), two
                )
        half //= 2
    return parts


def kernel(
    sizes, conc, mobility, kappa, well_depth, right_f, right_i, left_f, left_i, half_f, half_i, out,
    other, depths, other_depths, z_out, z_in, y_out, y_in, near, x_out, x_in, b_out, b_in, w_out, w_in,
    pair_send, pair_recv, zs, zr, ys, yr, xs, xr, bs, br, ws, wr,
):
    count_py, count_pz = sizes
    species, rows_x, rows_y, n = conc.shape
    me_sp, me_py, me_pz = lax.axis_index("sp"), lax.axis_index("py"), lax.axis_index("pz")
    blocks = count_pz * PIECES
    units = species * PIECES
    width = n // blocks
    groups = rows_x // blocks
    sub = SUBLANES
    slab_ky = blocks * sub
    slabs = n // slab_ky
    strip = rows_x * sub
    mesh_id = pl.DeviceIdType.MESH

    half = me_py // 2
    inner = lax.rem(me_py + half, 2) == 1
    outer = jnp.logical_not(inner)
    buddy = {"sp": me_sp, "py": me_py + 1 - 2 * lax.rem(me_py, 2), "pz": me_pz}
    across = {"sp": me_sp, "py": count_py - 1 - me_py, "pz": me_pz}

    def along_pz(step):
        return {"sp": me_sp, "py": me_py, "pz": lax.rem(me_pz + step, count_pz)}

    partner = {"sp": 1 - me_sp, "py": me_py, "pz": me_pz}
    barrier = pltpu.get_barrier_semaphore()
    peers = [partner, buddy]
    peers += [along_pz(step) for step in range(1, count_pz)]
    for peer in peers:
        pl.semaphore_signal(barrier, inc=1, device_id=peer, device_id_type=mesh_id)

    @pl.when(inner)
    def _():
        pl.semaphore_signal(barrier, inc=1, device_id=across, device_id_type=mesh_id)

    for t in range(species):
        depths[t : t + 1, :] = jnp.full((1, n), well_depth[t], jnp.float32)
    pl.semaphore_wait(barrier, len(peers) + jnp.where(inner, 1, 0))

    def remote(source, target, send, recv, peer):
        return pltpu.make_async_remote_copy(
            src_ref=source, dst_ref=target, send_sem=send, recv_sem=recv,
            device_id=peer, device_id_type=mesh_id,
        )

    pair = [
        remote(depths, other_depths, pair_send.at[0], pair_recv.at[0], partner),
        remote(conc, other, pair_send.at[1], pair_recv.at[1], partner),
    ]
    for copy in pair:
        copy.start()

    y_rows = pl.ds(pl.multiple_of(me_pz * rows_y, rows_y), rows_y)

    def z_copy(chunk, step):
        peer = lax.rem(me_pz + step, count_pz)
        return remote(
            z_out.at[chunk, peer], z_in.at[chunk, :, y_rows], zs.at[chunk, step],
            zr.at[chunk, step], along_pz(step),
        )

    def y_copy(chunk, slab):
        return remote(
            y_out.at[chunk, slab], y_in.at[chunk, slab], ys.at[chunk, slab],
            yr.at[chunk, slab], buddy,
        )

    def x_copy(one, slab):
        return remote(
            x_out.at[one, slab], x_in.at[one, slab], xs.at[one, slab], xr.at[one, slab], across
        )

    def b_copy(one, slab):
        return remote(
            b_out.at[one, slab], b_in.at[one, slab], bs.at[one, slab], br.at[one, slab], buddy
        )

    def w_copy(one, step):
        peer = lax.rem(me_pz + step, count_pz)
        return remote(
            w_out.at[one, peer], w_in.at[one, me_pz], ws.at[one, step],
            wr.at[one, step], along_pz(step),
        )

    for copy in pair:
        copy.wait_recv()

    def z_forward(one):
        own_i = me_sp * species + one
        terms = []
        for side, field, depth in ((me_sp, conc, depths), (1 - me_sp, other, other_depths)):
            for t in range(species):
                j = side * species + t
                weight = mobility[own_i, j]
                terms.append((field, t, weight * depth[t : t + 1, :], weight * kappa[j]))
        for g in range(groups):
            bulk_mix, conc_mix = [], []
            for block in range(blocks):
                first = second = None
                for field, t, bulk_weight, conc_weight in terms:
                    c = field[t, block * groups + g]
                    a = bulk_weight * (c * c * c - c)
                    b = conc_weight * c
                    first = a if first is None else first + a
                    second = b if second is None else second + b
                bulk_mix.append(first)
                conc_mix.append(second)
            modes = from_right(jnp.concatenate(bulk_mix + conc_mix, axis=0), right_f[...])
            modes = modes.reshape(2, blocks, rows_y, n)
            for f in range(2):
                swapped = swap_blocks([modes[f, block] for block in range(blocks)], width)
                for block in range(blocks):
                    unit = PIECES * one + block % PIECES
                    z_out[2 * unit + f, block // PIECES, g] = swapped[block]
        for c in range(2 * PIECES):
            for step in range(1, count_pz):
                z_copy(2 * PIECES * one + c, step).start()
        for c in range(2 * PIECES):
            chunk = 2 * PIECES * one + c
            z_in[chunk, :, y_rows] = z_out[chunk, me_pz]

    def y_chunk(chunk, _):
        for step in range(1, count_pz):
            z_copy(chunk, step).wait_recv()
        for g in range(0, groups, 2):
            lines = jnp.concatenate([z_in[chunk, g], z_in[chunk, g + 1]], axis=1)
            modes = from_left(left_f[...], lines)
            for h in range(2):
                part = modes[:, h * n : (h + 1) * n].reshape(slabs, blocks, sub, n)
                swapped = swap_blocks([part[:, b] for b in range(blocks)], width)
                for block in range(blocks):
                    start = (block * groups + g + h) * sub
                    y_out[chunk, :, start : start + sub, :] = swapped[block]
        return 0

    def y_forward(one):
        lax.fori_loop(2 * one, 2 * one + 2, y_chunk, 0)

        @pl.when(outer)
        def _():
            for slab in range(slabs):
                for f in range(2):
                    y_copy(2 * one + f, slab).start()

    def square(index):
        freq = jnp.minimum(index, n - index).astype(jnp.float32)
        root = freq * (2.0 * math.pi / n)
        return root * root

    lane = lax.broadcasted_iota(jnp.int32, (1, n), 1)
    ksq_x = square(lax.broadcasted_iota(jnp.int32, (n, 1), 0))

    def x_both(one, slab):
        for f in range(2):
            y_copy(2 * one + f, slab).wait_recv()
        own_i = me_sp * species + one // PIECES
        piece = me_pz * PIECES + lax.rem(one, PIECES)
        ksq_z = square(piece * width + lane % width)
        half_stiff = 0.5 * (mobility[own_i, own_i] * kappa[own_i])
        for r in range(0, sub, 2):
            both, ksq = [], []
            for f in range(2):
                chunk = 2 * one + f
                both.append(from_left(half_f[half], jnp.concatenate([
                    jnp.concatenate([
                        field[chunk, slab, pl.ds(r + h, rows_x, stride=sub), :]
                        for field in (y_out, y_in)
                    ], axis=0)
                    for h in range(2)
                ], axis=1)))
            for h in range(2):
                ksq_y = square(slab * slab_ky + (lane // width) * sub + (r + h))
                ksq.append(ksq_x + (ksq_y + ksq_z))
            ksq = jnp.concatenate(ksq, axis=1)
            drop = 0.5 * ksq * (both[0] + ksq * both[1]) / (1.0 + half_stiff * (ksq * ksq))
            lines = from_left(half_i[half], drop)
            for h in range(2):
                rows = pl.ds(r + h, n // 2, stride=sub)
                near[one, slab, rows, :] = lines[: n // 2, h * n : (h + 1) * n]
                x_out[one, slab, rows, :] = lines[n // 2 :, h * n : (h + 1) * n]
        x_copy(one, slab).start()

    def combine(one, slab):
        x_copy(one, slab).wait_recv()
        b_out[one, slab] = near[one, slab, strip:, :] + x_in[one, slab, strip:, :]
        b_copy(one, slab).start()
        b_in[one, slab] = near[one, slab, :strip, :] + x_in[one, slab, :strip, :]

    def y_back(one):
        @pl.when(outer)
        def _():
            for slab in range(slabs):
                b_copy(one, slab).wait_recv()

        for g in range(0, groups, 2):
            pairs = []
            for h in range(2):
                parts = []
                for block in range(blocks):
                    start = (block * groups + g + h) * sub
                    parts.append(b_in[one, :, start : start + sub, :])
                swapped = swap_blocks(parts, width)
                pairs.append(jnp.stack(swapped, axis=1).reshape(n, n))
            lines = from_left(left_i[...], jnp.concatenate(pairs, axis=1))
            for h in range(2):
                part = lines[:, h * n : (h + 1) * n].reshape(count_pz, rows_y, n)
                w_out[one, :, g + h] = part
        for step in range(1, count_pz):
            w_copy(one, step).start()
        w_in[one, me_pz] = w_out[one, me_pz]

    def z_back(one):
        for c in range(PIECES):
            for step in range(1, count_pz):
                w_copy(PIECES * one + c, step).wait_recv()
        for g in range(0, groups, 2):
            rows = []
            for h in range(2):
                rows += swap_blocks([
                    w_in[PIECES * one + block % PIECES, block // PIECES, g + h]
                    for block in range(blocks)
                ], width)
            lines = from_right(jnp.concatenate(rows, axis=0), right_i[...])
            lines = lines.reshape(2, blocks, rows_y, n)
            for h in range(2):
                for block in range(blocks):
                    x = block * groups + g + h
                    out[one, x] = conc[one, x] - lines[h, block]

    z_forward(0)
    y_forward(0)

    def opening(one, _):
        z_forward(one)
        return 0

    lax.fori_loop(1, species, opening, 0)
    y_forward(1)
    steps = units * slabs
    lag = 2

    def middle(k, _):
        @pl.when(jnp.logical_and(inner, k < steps))
        def _():
            x_both(k // slabs, lax.rem(k, slabs))

        for ahead in range(2):
            later = 2 * k + 2 + ahead

            @pl.when(later < units)
            def _():
                y_forward(later)

        back = k - lag

        @pl.when(jnp.logical_and(inner, jnp.logical_and(back >= 0, back < steps)))
        def _():
            combine(back // slabs, lax.rem(back, slabs))

        full = jnp.logical_and(back >= 0, lax.rem(back + 1, slabs) == 0)

        @pl.when(jnp.logical_and(full, back < steps))
        def _():
            y_back(back // slabs)

        done = back - 2 * slabs + 1
        whole = jnp.logical_and(done > 0, lax.rem(done, PIECES * slabs) == 0)

        @pl.when(whole)
        def _():
            z_back(done // (PIECES * slabs) - 1)

        return 0

    lax.fori_loop(0, steps + lag + 2 * slabs, middle, 0)

    for copy in pair:
        copy.wait_send()

    def drain(one, _):
        for step in range(1, count_pz):
            z_copy(2 * one, step).wait_send()
            z_copy(2 * one + 1, step).wait_send()
            w_copy(one, step).wait_send()

        @pl.when(outer)
        def _():
            for slab in range(slabs):
                y_copy(2 * one, slab).wait_send()
                y_copy(2 * one + 1, slab).wait_send()

        @pl.when(inner)
        def _():
            for slab in range(slabs):
                x_copy(one, slab).wait_send()
                b_copy(one, slab).wait_send()

        return 0

    lax.fori_loop(0, units, drain, 0)


def per_device_kernel(concentration, mobility, kappa, well_depth):
    species, rows_x, rows_y, n = concentration.shape
    count_py, count_pz = lax.axis_size("py"), lax.axis_size("pz")
    table = basis(n)
    forward = split_table(table)
    inverse = split_table(table.T)
    blocks = np.arange(n).reshape(count_py, rows_x)
    orders = [blocks[[1, 0, 2, 3]].reshape(n), blocks[[2, 3, 1, 0]].reshape(n)]
    half_forward = np.stack([split_table(table[order[: n // 2]]).T for order in orders])
    half_inverse = np.stack([split_table(table[order].T).T for order in orders])
    blocks = count_pz * PIECES
    units = species * PIECES
    groups = rows_x // blocks
    slabs = n // (blocks * SUBLANES)
    strip = rows_x * SUBLANES
    f32 = jnp.float32
    vmem = pl.BlockSpec(memory_space=pltpu.VMEM)
    smem = pl.BlockSpec(memory_space=pltpu.SMEM)
    dma = pltpu.SemaphoreType.DMA
    return pl.pallas_call(
        functools.partial(kernel, (count_py, count_pz)),
        out_shape=jax.ShapeDtypeStruct(concentration.shape, f32),
        in_specs=[vmem, smem, smem, smem] + [vmem] * 6,
        out_specs=vmem,
        scratch_shapes=[
            pltpu.VMEM((species, rows_x, rows_y, n), f32),
            pltpu.VMEM((species, n), f32),
            pltpu.VMEM((species, n), f32),
            pltpu.VMEM((2 * units, count_pz, groups, rows_y, n), f32),
            pltpu.VMEM((2 * units, groups, n, n), f32),
            pltpu.VMEM((2 * units, slabs, strip, n), f32),
            pltpu.VMEM((2 * units, slabs, strip, n), f32),
            pltpu.VMEM((units, slabs, 2 * strip, n), f32),
            pltpu.VMEM((units, slabs, 2 * strip, n), f32),
            pltpu.VMEM((units, slabs, 2 * strip, n), f32),
            pltpu.VMEM((units, slabs, strip, n), f32),
            pltpu.VMEM((units, slabs, strip, n), f32),
            pltpu.VMEM((units, count_pz, groups, rows_y, n), f32),
            pltpu.VMEM((units, count_pz, groups, rows_y, n), f32),
            dma((2,)), dma((2,)),
            dma((2 * units, count_pz)), dma((2 * units, count_pz)),
            dma((2 * units, slabs)), dma((2 * units, slabs)),
            dma((units, slabs)), dma((units, slabs)),
            dma((units, slabs)), dma((units, slabs)),
            dma((units, count_pz)), dma((units, count_pz)),
        ],
        compiler_params=pltpu.CompilerParams(
            collective_id=0, has_side_effects=True, vmem_limit_bytes=60 * 1024 * 1024
        ),
        name="step",
    )(
        concentration, mobility, kappa, well_depth,
        jnp.asarray(forward), jnp.asarray(inverse),
        jnp.asarray(forward.T), jnp.asarray(inverse.T),
        jnp.asarray(half_forward), jnp.asarray(half_inverse),
    )


def per_device(concentration, mobility, kappa, well_depth):
    rows_x, rows_y, n = concentration.shape[1:]
    count_sp, count_py, count_pz = (lax.axis_size(name) for name in ("sp", "py", "pz"))
    cube = rows_x * count_py == n and rows_y * count_pz == n and n == 128
    power = count_pz > 1 and count_pz & (count_pz - 1) == 0
    blocks = count_pz * PIECES
    whole = n % (SUBLANES * blocks) == 0 and rows_x % (2 * blocks) == 0 and rows_y % SUBLANES == 0
    if cube and power and whole and count_sp == 2 and count_py == 4:
        return per_device_kernel(concentration, mobility, kappa, well_depth)
    return per_device_general(concentration, mobility, kappa, well_depth)


def solution(mesh):
    in_specs = (P("sp", "py", "pz", None), P(), P(), P("sp"))
    out_specs = P("sp", "py", "pz", None)
    return jax.shard_map(
        per_device, mesh=mesh, in_specs=in_specs, out_specs=out_specs, check_vma=False
    )
```

profile of v0, /device:TPU:0, one launch (start us, length us, event | category | flops | bytes accessed | tf_op | source)
XLA Modules:
  0.0 139.7 jit_solution(896279712163336944)
XLA Ops:
  0.0 136.6 %step.1 = f32[4,32,32,128]{3,2,1,0:T(8,128)} custom-call(f32[4,32,32,128]{3,2,1,0:T(8,128)} %conc.1, f32[8,8]{1,0:T(8,128)} %mobility.1, f32[8]{0:T(128)} %kappa.1, f32[4]{0:T(128)} %well_depth.1, bf16[256,256]{1,0:T(8,128)(2,1)} %constant.12.clone.right_f, bf16[256,256]{1,0:T(8,128)(2,1)} %constant.13.clone.right_i, ...), custom_call_target="tpu_custom_call" | custom-call | tf_op jit(solution)/shard_map/step/pallas_call | solution.py:500
  136.6 3.1 %copy.12 = f32[4,32,32,128]{3,2,1,0:T(8,128)} copy(f32[4,32,32,128]{3,2,1,0:T(8,128)} %step.1) | data formatting | bytes 4194304
where the time goes:
time: 140 us
  Pallas kernels  137 us (98%)
  local copies, waits for them, and re-layouts  3.08 us (2%)
    pallas_call x1, Pallas kernels, per_device_kernel(): pl.pallas_call(functools.partial(kernel, (count_py, count_pz)), out_shape...  137 us
    unnamed x1, local copies, waits for them, and re-layouts  3.08 us

commit v1 on v0

--- a/solution.py
+++ b/solution.py
@@ -174,9 +174,12 @@
 
 
 def kernel(
-    sizes, conc, mobility, kappa, well_depth, right_f, right_i, left_f, left_i, half_f, half_i, out,
+    sizes, conc_hbm, mobility, kappa, well_depth, right_f_hbm, right_i_hbm, left_f_hbm, left_i_hbm,
+    half_f_hbm, half_i_hbm, out,
+    conc, right_f, right_i, left_f, left_i, half_f, half_i, own_mix,
     other, depths, other_depths, z_out, z_in, y_out, y_in, near, x_out, x_in, b_out, b_in, w_out, w_in,
-    pair_send, pair_recv, zs, zr, ys, yr, xs, xr, bs, br, ws, wr,
+    load, table_load, pair_send, pair_recv, depth_send, depth_recv,
+    zs, zr, ys, yr, xs, xr, bs, br, ws, wr,
 ):
     count_py, count_pz = sizes
     species, rows_x, rows_y, n = conc.shape
@@ -186,8 +189,6 @@
     width = n // blocks
     groups = rows_x // blocks
     sub = SUBLANES
-    slab_ky = blocks * sub
-    slabs = n // slab_ky
     strip = rows_x * sub
     mesh_id = pl.DeviceIdType.MESH
 
@@ -211,8 +212,26 @@
     def _():
         pl.semaphore_signal(barrier, inc=1, device_id=across, device_id_type=mesh_id)
 
+    def lot(g):
+        return pl.ds(g * blocks, blocks)
+
+    loads = [
+        pltpu.make_async_copy(conc_hbm.at[:, lot(g)], conc.at[:, lot(g)], load.at[g])
+        for g in range(groups)
+    ]
+    table_loads = [
+        pltpu.make_async_copy(source, target, table_load.at[i])
+        for i, (source, target) in enumerate([
+            (right_f_hbm, right_f), (left_f_hbm, left_f), (half_f_hbm.at[half], half_f),
+            (half_i_hbm.at[half], half_i), (left_i_hbm, left_i), (right_i_hbm, right_i),
+        ])
+    ]
+    for copy in loads + table_loads:
+        copy.start()
     for t in range(species):
         depths[t : t + 1, :] = jnp.full((1, n), well_depth[t], jnp.float32)
+    for copy in loads:
+        copy.wait()
     pl.semaphore_wait(barrier, len(peers) + jnp.where(inner, 1, 0))
 
     def remote(source, target, send, recv, peer):
@@ -221,66 +240,89 @@
             device_id=peer, device_id_type=mesh_id,
         )
 
+    depth_pair = remote(depths, other_depths, depth_send, depth_recv, partner)
     pair = [
-        remote(depths, other_depths, pair_send.at[0], pair_recv.at[0], partner),
-        remote(conc, other, pair_send.at[1], pair_recv.at[1], partner),
+        remote(
+            conc.at[:, lot(g)], other.at[:, lot(g)], pair_send.at[g], pair_recv.at[g], partner
+        )
+        for g in range(groups)
     ]
+    depth_pair.start()
     for copy in pair:
         copy.start()
 
     y_rows = pl.ds(pl.multiple_of(me_pz * rows_y, rows_y), rows_y)
 
-    def z_copy(chunk, step):
+    def z_copy(chunk, step, part):
         peer = lax.rem(me_pz + step, count_pz)
         return remote(
-            z_out.at[chunk, peer], z_in.at[chunk, :, y_rows], zs.at[chunk, step],
-            zr.at[chunk, step], along_pz(step),
+            z_out.at[chunk, peer, part], z_in.at[chunk, part, y_rows], zs.at[0],
+            zr.at[chunk], along_pz(step),
         )
 
-    def y_copy(chunk, slab):
+    def z_all(chunk):
+        lines = z_in.at[chunk, :, pl.ds(0, (count_pz - 1) * rows_y)]
+        return remote(lines, lines, zs.at[0], zr.at[chunk], partner)
+
+    def y_copy(chunk):
+        return remote(y_out.at[chunk], y_in.at[chunk], ys.at[0], yr.at[chunk], buddy)
+
+    near_strip, far_strip = pl.ds(0, strip), pl.ds(strip, strip)
+
+    def x_copy(one, part):
+        rows = far_strip if part == 0 else near_strip
         return remote(
-            y_out.at[chunk, slab], y_in.at[chunk, slab], ys.at[chunk, slab],
-            yr.at[chunk, slab], buddy,
+            x_out.at[one, rows], x_in.at[one, rows], xs.at[0], xr.at[one, part], across
         )
 
-    def x_copy(one, slab):
-        return remote(
-            x_out.at[one, slab], x_in.at[one, slab], xs.at[one, slab], xr.at[one, slab], across
-        )
-
-    def b_copy(one, slab):
-        return remote(
-            b_out.at[one, slab], b_in.at[one, slab], bs.at[one, slab], br.at[one, slab], buddy
-        )
+    def b_copy(one):
+        return remote(b_out.at[one], b_in.at[one], bs.at[0], br.at[one], buddy)
 
     def w_copy(one, step):
         peer = lax.rem(me_pz + step, count_pz)
         return remote(
-            w_out.at[one, peer], w_in.at[one, me_pz], ws.at[one, step],
-            wr.at[one, step], along_pz(step),
+            w_out.at[one, peer], w_in.at[one, me_pz], ws.at[0], wr.at[one], along_pz(step),
         )
 
-    for copy in pair:
-        copy.wait_recv()
-
-    def z_forward(one):
+    def w_all(one):
+        lines = w_in.at[one, pl.ds(0, count_pz - 1)]
+        return remote(lines, lines, ws.at[0], wr.at[one], partner)
+
+    def terms_of(one, side, field, depth):
         own_i = me_sp * species + one
         terms = []
-        for side, field, depth in ((me_sp, conc, depths), (1 - me_sp, other, other_depths)):
-            for t in range(species):
-                j = side * species + t
-                weight = mobility[own_i, j]
-                terms.append((field, t, weight * depth[t : t + 1, :], weight * kappa[j]))
+        for t in range(species):
+            j = side * species + t
+            weight = mobility[own_i, j]
+            terms.append((field, t, weight * depth[t : t + 1, :], weight * kappa[j]))
+        return terms
+
+    def mixed(terms, x, first=None, second=None):
+        for field, t, bulk_weight, conc_weight in terms:
+            c = field[t, x]
+            a = bulk_weight * (c * c * c - c)
+            b = conc_weight * c
+            first = a if first is None else first + a
+            second = b if second is None else second + b
+        return first, second
+
+    def z_forward(one, opening=False):
+        own = terms_of(one, me_sp, conc, depths)
+        if opening:
+            for x in range(rows_x):
+                own_mix[0, x], own_mix[1, x] = mixed(own, x)
+            depth_pair.wait_recv()
+        others = terms_of(one, 1 - me_sp, other, other_depths)
         for g in range(groups):
+            if opening:
+                pair[g].wait_recv()
             bulk_mix, conc_mix = [], []
             for block in range(blocks):
-                first = second = None
-                for field, t, bulk_weight, conc_weight in terms:
-                    c = field[t, block * groups + g]
-                    a = bulk_weight * (c * c * c - c)
-                    b = conc_weight * c
-                    first = a if first is None else first + a
-                    second = b if second is None else second + b
+                x = g * blocks + block
+                if opening:
+                    first, second = mixed(others, x, own_mix[0, x], own_mix[1, x])
+                else:
+                    first, second = mixed(own + others, x)
                 bulk_mix.append(first)
                 conc_mix.append(second)
             modes = from_right(jnp.concatenate(bulk_mix + conc_mix, axis=0), right_f[...])
@@ -290,35 +332,37 @@
                 for block in range(blocks):
                     unit = PIECES * one + block % PIECES
                     z_out[2 * unit + f, block // PIECES, g] = swapped[block]
-        for c in range(2 * PIECES):
+            if opening:
+                for c in range(2):
+                    for step in range(1, count_pz):
+                        z_copy(c, step, pl.ds(g, 1)).start()
+        for c in range(2 if opening else 0, 2 * PIECES):
             for step in range(1, count_pz):
-                z_copy(2 * PIECES * one + c, step).start()
+                z_copy(2 * PIECES * one + c, step, pl.ds(0, groups)).start()
         for c in range(2 * PIECES):
             chunk = 2 * PIECES * one + c
             z_in[chunk, :, y_rows] = z_out[chunk, me_pz]
 
     def y_chunk(chunk, _):
-        for step in range(1, count_pz):
-            z_copy(chunk, step).wait_recv()
+        z_all(chunk).wait_recv()
         for g in range(0, groups, 2):
             lines = jnp.concatenate([z_in[chunk, g], z_in[chunk, g + 1]], axis=1)
             modes = from_left(left_f[...], lines)
             for h in range(2):
-                part = modes[:, h * n : (h + 1) * n].reshape(slabs, blocks, sub, n)
-                swapped = swap_blocks([part[:, b] for b in range(blocks)], width)
+                part = modes[:, h * n : (h + 1) * n].reshape(blocks, sub, n)
+                swapped = swap_blocks([part[b] for b in range(blocks)], width)
                 for block in range(blocks):
-                    start = (block * groups + g + h) * sub
-                    y_out[chunk, :, start : start + sub, :] = swapped[block]
+                    start = ((g + h) * blocks + block) * sub
+                    y_out[chunk, start : start + sub, :] = swapped[block]
+
+        @pl.when(outer)
+        def _():
+            y_copy(chunk).start()
+
         return 0
 
     def y_forward(one):
         lax.fori_loop(2 * one, 2 * one + 2, y_chunk, 0)
-
-        @pl.when(outer)
-        def _():
-            for slab in range(slabs):
-                for f in range(2):
-                    y_copy(2 * one + f, slab).start()
 
     def square(index):
         freq = jnp.minimum(index, n - index).astype(jnp.float32)
@@ -328,9 +372,9 @@
     lane = lax.broadcasted_iota(jnp.int32, (1, n), 1)
     ksq_x = square(lax.broadcasted_iota(jnp.int32, (n, 1), 0))
 
-    def x_both(one, slab):
+    def x_both(one):
         for f in range(2):
-            y_copy(2 * one + f, slab).wait_recv()
+            y_copy(2 * one + f).wait_recv()
         own_i = me_sp * species + one // PIECES
         piece = me_pz * PIECES + lax.rem(one, PIECES)
         ksq_z = square(piece * width + lane % width)
@@ -339,46 +383,47 @@
             both, ksq = [], []
             for f in range(2):
                 chunk = 2 * one + f
-                both.append(from_left(half_f[half], jnp.concatenate([
+                both.append(from_left(half_f[...], jnp.concatenate([
                     jnp.concatenate([
-                        field[chunk, slab, pl.ds(r + h, rows_x, stride=sub), :]
+                        field[chunk, pl.ds(r + h, rows_x, stride=sub), :]
                         for field in (y_out, y_in)
                     ], axis=0)
                     for h in range(2)
                 ], axis=1)))
             for h in range(2):
-                ksq_y = square(slab * slab_ky + (lane // width) * sub + (r + h))
+                ksq_y = square((lane // width) * sub + (r + h))
                 ksq.append(ksq_x + (ksq_y + ksq_z))
             ksq = jnp.concatenate(ksq, axis=1)
             drop = 0.5 * ksq * (both[0] + ksq * both[1]) / (1.0 + half_stiff * (ksq * ksq))
-            lines = from_left(half_i[half], drop)
+            lines = from_left(half_i[...], drop)
             for h in range(2):
                 rows = pl.ds(r + h, n // 2, stride=sub)
-                near[one, slab, rows, :] = lines[: n // 2, h * n : (h + 1) * n]
-                x_out[one, slab, rows, :] = lines[n // 2 :, h * n : (h + 1) * n]
-        x_copy(one, slab).start()
-
-    def combine(one, slab):
-        x_copy(one, slab).wait_recv()
-        b_out[one, slab] = near[one, slab, strip:, :] + x_in[one, slab, strip:, :]
-        b_copy(one, slab).start()
-        b_in[one, slab] = near[one, slab, :strip, :] + x_in[one, slab, :strip, :]
+                near[one, rows, :] = lines[: n // 2, h * n : (h + 1) * n]
+                x_out[one, rows, :] = lines[n // 2 :, h * n : (h + 1) * n]
+        for part in range(2):
+            x_copy(one, part).start()
+
+    def combine(one):
+        x_copy(one, 0).wait_recv()
+        b_out[one] = near[one, strip:, :] + x_in[one, strip:, :]
+        b_copy(one).start()
+        x_copy(one, 1).wait_recv()
+        b_in[one] = near[one, :strip, :] + x_in[one, :strip, :]
 
     def y_back(one):
         @pl.when(outer)
         def _():
-            for slab in range(slabs):
-                b_copy(one, slab).wait_recv()
+            b_copy(one).wait_recv()
 
         for g in range(0, groups, 2):
             pairs = []
             for h in range(2):
                 parts = []
                 for block in range(blocks):
-                    start = (block * groups + g + h) * sub
-                    parts.append(b_in[one, :, start : start + sub, :])
+                    start = ((g + h) * blocks + block) * sub
+                    parts.append(b_in[one, start : start + sub, :])
                 swapped = swap_blocks(parts, width)
-                pairs.append(jnp.stack(swapped, axis=1).reshape(n, n))
+                pairs.append(jnp.stack(swapped, axis=0).reshape(n, n))
             lines = from_left(left_i[...], jnp.concatenate(pairs, axis=1))
             for h in range(2):
                 part = lines[:, h * n : (h + 1) * n].reshape(count_pz, rows_y, n)
@@ -389,8 +434,7 @@
 
     def z_back(one):
         for c in range(PIECES):
-            for step in range(1, count_pz):
-                w_copy(PIECES * one + c, step).wait_recv()
+            w_all(PIECES * one + c).wait_recv()
         for g in range(0, groups, 2):
             rows = []
             for h in range(2):
@@ -402,25 +446,27 @@
             lines = lines.reshape(2, blocks, rows_y, n)
             for h in range(2):
                 for block in range(blocks):
-                    x = block * groups + g + h
+                    x = (g + h) * blocks + block
                     out[one, x] = conc[one, x] - lines[h, block]
 
-    z_forward(0)
+    table_loads[0].wait()
+    z_forward(0, True)
+    for copy in table_loads[1:]:
+        copy.wait()
+    z_forward(1)
     y_forward(0)
-
-    def opening(one, _):
-        z_forward(one)
-        return 0
-
-    lax.fori_loop(1, species, opening, 0)
     y_forward(1)
-    steps = units * slabs
+    z_forward(2)
     lag = 2
 
     def middle(k, _):
-        @pl.when(jnp.logical_and(inner, k < steps))
+        @pl.when(jnp.logical_and(inner, k < units))
         def _():
-            x_both(k // slabs, lax.rem(k, slabs))
+            x_both(k)
+
+        @pl.when(k == 1)
+        def _():
+            z_forward(3)
 
         for ahead in range(2):
             later = 2 * k + 2 + ahead
@@ -431,51 +477,41 @@
 
         back = k - lag
 
-        @pl.when(jnp.logical_and(inner, jnp.logical_and(back >= 0, back < steps)))
+        @pl.when(jnp.logical_and(inner, jnp.logical_and(back >= 0, back < units)))
         def _():
-            combine(back // slabs, lax.rem(back, slabs))
-
-        full = jnp.logical_and(back >= 0, lax.rem(back + 1, slabs) == 0)
-
-        @pl.when(jnp.logical_and(full, back < steps))
+            combine(back)
+
+        @pl.when(jnp.logical_and(back >= 0, back < units))
         def _():
-            y_back(back // slabs)
-
-        done = back - 2 * slabs + 1
-        whole = jnp.logical_and(done > 0, lax.rem(done, PIECES * slabs) == 0)
+            y_back(back)
+
+        done = back - 1
+        whole = jnp.logical_and(done > 0, lax.rem(done, PIECES) == 0)
 
         @pl.when(whole)
         def _():
-            z_back(done // (PIECES * slabs) - 1)
+            z_back(done // PIECES - 1)
 
         return 0
 
-    lax.fori_loop(0, steps + lag + 2 * slabs, middle, 0)
-
+    lax.fori_loop(0, units + lag + 2, middle, 0)
+
+    depth_pair.wait_send()
     for copy in pair:
         copy.wait_send()
-
-    def drain(one, _):
-        for step in range(1, count_pz):
-            z_copy(2 * one, step).wait_send()
-            z_copy(2 * one + 1, step).wait_send()
-            w_copy(one, step).wait_send()
-
-        @pl.when(outer)
-        def _():
-            for slab in range(slabs):
-                y_copy(2 * one, slab).wait_send()
-                y_copy(2 * one + 1, slab).wait_send()
-
-        @pl.when(inner)
-        def _():
-            for slab in range(slabs):
-                x_copy(one, slab).wait_send()
-                b_copy(one, slab).wait_send()
-
-        return 0
-
-    lax.fori_loop(0, units, drain, 0)
+    sent = z_out.at[:, pl.ds(0, count_pz - 1)]
+    remote(sent, sent, zs.at[0], zr.at[0], partner).wait_send()
+    sent = w_out.at[:, pl.ds(0, count_pz - 1)]
+    remote(sent, sent, ws.at[0], wr.at[0], partner).wait_send()
+
+    @pl.when(outer)
+    def _():
+        remote(y_out, y_in, ys.at[0], yr.at[0], buddy).wait_send()
+
+    @pl.when(inner)
+    def _():
+        remote(x_out, x_in, xs.at[0], xr.at[0, 0], across).wait_send()
+        remote(b_out, b_in, bs.at[0], br.at[0], buddy).wait_send()
 
 
 def per_device_kernel(concentration, mobility, kappa, well_depth):
@@ -491,59 +527,72 @@
     blocks = count_pz * PIECES
     units = species * PIECES
     groups = rows_x // blocks
-    slabs = n // (blocks * SUBLANES)
     strip = rows_x * SUBLANES
-    f32 = jnp.float32
+    f32, bf16 = jnp.float32, jnp.bfloat16
     vmem = pl.BlockSpec(memory_space=pltpu.VMEM)
     smem = pl.BlockSpec(memory_space=pltpu.SMEM)
+    hbm = pl.BlockSpec(memory_space=pltpu.HBM)
     dma = pltpu.SemaphoreType.DMA
+
+    def far(array):
+        return pltpu.with_memory_space_constraint(array, pltpu.HBM)
+
     return pl.pallas_call(
         functools.partial(kernel, (count_py, count_pz)),
         out_shape=jax.ShapeDtypeStruct(concentration.shape, f32),
-        in_specs=[vmem, smem, smem, smem] + [vmem] * 6,
+        in_specs=[hbm, smem, smem, smem] + [hbm] * 6,
         out_specs=vmem,
         scratch_shapes=[
+            pltpu.VMEM((species, rows_x, rows_y, n), f32),
+            pltpu.VMEM(forward.shape, bf16),
+            pltpu.VMEM(inverse.shape, bf16),
+            pltpu.VMEM(forward.T.shape, bf16),
+            pltpu.VMEM(inverse.T.shape, bf16),
+            pltpu.VMEM(half_forward.shape[1:], bf16),
+            pltpu.VMEM(half_inverse.shape[1:], bf16),
+            pltpu.VMEM((2, rows_x, rows_y, n), f32),
             pltpu.VMEM((species, rows_x, rows_y, n), f32),
             pltpu.VMEM((species, n), f32),
             pltpu.VMEM((species, n), f32),
             pltpu.VMEM((2 * units, count_pz, groups, rows_y, n), f32),
             pltpu.VMEM((2 * units, groups, n, n), f32),
-            pltpu.VMEM((2 * units, slabs, strip, n), f32),
-            pltpu.VMEM((2 * units, slabs, strip, n), f32),
-            pltpu.VMEM((units, slabs, 2 * strip, n), f32),
-            pltpu.VMEM((units, slabs, 2 * strip, n), f32),
-            pltpu.VMEM((units, slabs, 2 * strip, n), f32),
-            pltpu.VMEM((units, slabs, strip, n), f32),
-            pltpu.VMEM((units, slabs, strip, n), f32),
+            pltpu.VMEM((2 * units, strip, n), f32),
+            pltpu.VMEM((2 * units, strip, n), f32),
+            pltpu.VMEM((units, 2 * strip, n), f32),
+            pltpu.VMEM((units, 2 * strip, n), f32),
+            pltpu.VMEM((units, 2 * strip, n), f32),
+            pltpu.VMEM((units, strip, n), f32),
+            pltpu.VMEM((units, strip, n), f32),
             pltpu.VMEM((units, count_pz, groups, rows_y, n), f32),
             pltpu.VMEM((units, count_pz, groups, rows_y, n), f32),
-            dma((2,)), dma((2,)),
-            dma((2 * units, count_pz)), dma((2 * units, count_pz)),
-            dma((2 * units, slabs)), dma((2 * units, slabs)),
-            dma((units, slabs)), dma((units, slabs)),
-            dma((units, slabs)), dma((units, slabs)),
-            dma((units, count_pz)), dma((units, count_pz)),
+            dma((groups,)), dma((6,)),
+            dma((groups,)), dma((groups,)), dma, dma,
+            dma((1,)), dma((2 * units,)),
+            dma((1,)), dma((2 * units,)),
+            dma((1,)), dma((units, 2)),
+            dma((1,)), dma((units,)),
+            dma((1,)), dma((units,)),
         ],
         compiler_params=pltpu.CompilerParams(
-            collective_id=0, has_side_effects=True, vmem_limit_bytes=60 * 1024 * 1024
+            collective_id=0, has_side_effects=True, vmem_limit_bytes=46 * 1024 * 1024
         ),
         name="step",
     )(
-        concentration, mobility, kappa, well_depth,
-        jnp.asarray(forward), jnp.asarray(inverse),
-        jnp.asarray(forward.T), jnp.asarray(inverse.T),
-        jnp.asarray(half_forward), jnp.asarray(half_inverse),
+        far(concentration), far(mobility), far(kappa), far(well_depth),
+        *(far(jnp.asarray(each)) for each in (
+            forward, inverse, forward.T, inverse.T, half_forward, half_inverse
+        )),
     )
 
 
 def per_device(concentration, mobility, kappa, well_depth):
-    rows_x, rows_y, n = concentration.shape[1:]
+    species, rows_x, rows_y, n = concentration.shape
     count_sp, count_py, count_pz = (lax.axis_size(name) for name in ("sp", "py", "pz"))
     cube = rows_x * count_py == n and rows_y * count_pz == n and n == 128
     power = count_pz > 1 and count_pz & (count_pz - 1) == 0
     blocks = count_pz * PIECES
-    whole = n % (SUBLANES * blocks) == 0 and rows_x % (2 * blocks) == 0 and rows_y % SUBLANES == 0
-    if cube and power and whole and count_sp == 2 and count_py == 4:
+    whole = n == SUBLANES * blocks and rows_x % (2 * blocks) == 0 and rows_y % SUBLANES == 0
+    if cube and power and whole and count_sp == 2 and count_py == 4 and species == 4:
         return per_device_kernel(concentration, mobility, kappa, well_depth)
     return per_device_general(concentration, mobility, kappa, well_depth)
 

time: 140 us -> 125 us (0.89)
  Pallas kernels: 137 us -> 124 us
  local copies, waits for them, and re-layouts: 3.08 us -> 1.32 us
    pallas_call x1, Pallas kernels: 137 us -> 124 us  [per_device_kernel(): pl.pallas_call(functools.partial(kernel, (count_py, count_pz)), out_shape...]
    unnamed x1, local copies, waits for them, and re-layouts: 3.08 us -> 1.32 us
where the time goes in v1:
time: 125 us
  Pallas kernels  124 us (99%)
  local copies, waits for them, and re-layouts  1.32 us (1%)
    pallas_call x1, Pallas kernels, per_device_kernel(): pl.pallas_call(functools.partial(kernel, (count_py, count_pz)), out_shape...  124 us

profile of v1, /device:TPU:0, one launch (start us, length us, event | category | flops | bytes accessed | tf_op | source)
XLA Modules:
  0.0 124.8 jit_solution(5264356880907580345)
XLA Ops:
  0.0 123.5 %step.1 = f32[4,32,32,128]{3,2,1,0:T(8,128)S(1)} custom-call(f32[4,32,32,128]{3,2,1,0:T(8,128)} %conc_hbm.1, f32[8,8]{1,0:T(8,128)} %mobility.1, f32[8]{0:T(128)} %kappa.1, f32[4]{0:T(128)} %well_depth.1, bf16[256,256]{1,0:T(8,128)(2,1)} %constant.12.clone.right_f_hbm, bf16[256,256]{1,0:T(8,128)(2,1)} %constant.13.clone.right_i_hbm, ...), custom_call_target="tpu_custom_call" | custom-call | tf_op jit(solution)/shard_map/step/pallas_call | solution.py:540
  123.5 1.3 %copy.12 = f32[4,32,32,128]{3,2,1,0:T(8,128)} copy(f32[4,32,32,128]{3,2,1,0:T(8,128)S(1)} %step.1) | data formatting | bytes 4194304

commit v2 on v1

v2 whole, which is shorter than its diff:
```python
import functools
import math

import jax
import jax.numpy as jnp
import numpy as np
from jax import lax
from jax.experimental import pallas as pl
from jax.experimental.pallas import tpu as pltpu
from jax.sharding import PartitionSpec as P


def tables(count):
    modes = jnp.arange(count, dtype=jnp.int32)
    product = modes[:, None] * modes[None, :] % count
    angle = 2.0 * math.pi * product.astype(jnp.float32) / count
    return (jnp.cos(angle), jnp.sin(angle))


def wave_square(index, count):
    freq = jnp.where(index < count // 2, index, index - count).astype(jnp.float32)
    return (2.0 * math.pi * freq / count) ** 2


def contract(form, values, table):
    return jnp.einsum(form, values, table, precision=lax.Precision.HIGHEST)


def rotate(spectrum, form, count, forward):
    cosine, sine = tables(count)
    real_part, imag_part = (spectrum[0], spectrum[1])
    real_cos = contract(form, real_part, cosine)
    real_sin = contract(form, real_part, sine)
    imag_cos = contract(form, imag_part, cosine)
    imag_sin = contract(form, imag_part, sine)
    if forward:
        return jnp.stack([real_cos + imag_sin, imag_cos - real_sin])
    return jnp.stack([real_cos - imag_sin, imag_cos + real_sin])


def per_device_general(concentration, mobility, kappa, well_depth):
    local_species, rows_x, rows_y, depth = concentration.shape
    count_sp = lax.axis_size("sp")
    count_py = lax.axis_size("py")
    count_pz = lax.axis_size("pz")
    full_x = rows_x * count_py
    full_y = rows_y * count_pz
    half_depth = depth // 2
    bulk = well_depth[:, None, None, None] * (
        concentration * concentration * concentration - concentration
    )
    fields = jnp.stack([concentration, bulk])
    cosine, sine = tables(depth)
    alternate = (1 - 2 * (jnp.arange(depth, dtype=jnp.int32) % 2)).astype(jnp.float32)
    spectrum = jnp.stack(
        [
            contract("fsxyz,zk->fsxyk", fields, cosine[:, :half_depth]),
            -contract("fsxyz,zk->fsxyk", fields, sine[:, :half_depth]),
        ]
    )
    spectrum = lax.all_to_all(spectrum, "pz", split_axis=5, concat_axis=4, tiled=True)
    own_lines = spectrum.shape[5]
    highest = contract("fsxyz,z->fsxy", fields, alternate)
    highest = lax.all_gather(highest, "pz", axis=3, tiled=True)
    highest = jnp.stack([highest, jnp.zeros_like(highest)])[..., None]
    spectrum = jnp.concatenate([spectrum, highest], axis=5)
    z_modes = jnp.concatenate(
        [
            lax.axis_index("pz") * own_lines + jnp.arange(own_lines, dtype=jnp.int32),
            jnp.full((1,), half_depth, jnp.int32),
        ]
    )
    spectrum = rotate(spectrum, "fsxyz,yk->fsxkz", full_y, True)
    spectrum = lax.all_to_all(
        lax.all_to_all(spectrum, "sp", split_axis=4, concat_axis=2, tiled=True),
        "py",
        split_axis=4,
        concat_axis=3,
        tiled=True,
    )
    spectrum = rotate(spectrum, "fsxyz,xk->fskyz", full_x, True)
    narrow = spectrum.shape[4]
    lines = spectrum.shape[5]
    y_start = (lax.axis_index("sp") * count_py + lax.axis_index("py")) * narrow
    ksq_x = wave_square(jnp.arange(full_x, dtype=jnp.int32), full_x)
    ksq_y = wave_square(y_start + jnp.arange(narrow, dtype=jnp.int32), full_y)
    ksq_z = wave_square(z_modes, depth)
    ksq = ksq_x[:, None, None] + ksq_y[None, :, None] + ksq_z[None, None, :]
    c_hat = spectrum[:, 0]
    drive = spectrum[:, 1] + kappa[None, :, None, None, None] * ksq[None, None] * c_hat
    mix = jnp.einsum("ij,rjxyz->rixyz", mobility, drive, precision=lax.Precision.HIGHEST)
    stiff = 0.5 * (jnp.diagonal(mobility) * kappa)[:, None, None, None] * (ksq * ksq)[None]
    new_hat = (c_hat * (1.0 + stiff)[None] - 0.5 * ksq[None, None] * mix) / (1.0 + stiff)[None]
    new_hat = rotate(new_hat, "sxyz,xk->skyz", full_x, False)
    moved = lax.all_to_all(
        lax.all_to_all(new_hat, "sp", split_axis=1, concat_axis=3, tiled=True),
        "py",
        split_axis=2,
        concat_axis=3,
        tiled=True,
    )
    moved = moved.reshape(2, local_species, rows_x, count_py, count_sp, narrow, lines)
    moved = moved.transpose(0, 1, 2, 4, 3, 5, 6).reshape(2, local_species, rows_x, full_y, lines)
    moved = rotate(moved, "sxyz,yk->sxkz", full_y, False)
    main = moved[..., : lines - 1]
    highest = moved[0, :, :, :, lines - 1]
    main = lax.all_to_all(main, "pz", split_axis=3, concat_axis=4, tiled=True)
    highest = lax.dynamic_slice_in_dim(highest, lax.axis_index("pz") * rows_y, rows_y, 2)
    weight = jnp.where(jnp.arange(half_depth, dtype=jnp.int32) == 0, 1.0, 2.0).astype(jnp.float32)
    result = contract("sxyk,kz->sxyz", main[0] * weight, cosine[:half_depth]) - contract(
        "sxyk,kz->sxyz", main[1] * weight, sine[:half_depth]
    )
    result = result + highest[..., None] * alternate[None, None, None, :]
    return result * (1.0 / (full_x * full_y * depth))


PIECES = 4
SUBLANES = 8
SLOTS = 6


def basis(count):
    grid = np.arange(count)
    mode = np.arange(count)
    freq = np.minimum(mode, count - mode)
    angle = 2.0 * np.pi * (grid[:, None] * freq[None, :] % count) / count
    table = np.where(mode[None, :] <= count // 2, np.cos(angle), np.sin(angle))
    single = (mode == 0) | (2 * mode == count)
    return table * np.sqrt(np.where(single, 1.0, 2.0) / count)[None, :]


def split_table(table):
    table = table.astype(np.float32)
    high = table.astype(jnp.bfloat16)
    low = (table - high.astype(np.float32)).astype(jnp.bfloat16)
    row = np.concatenate([high, low], axis=1)
    return np.concatenate([row, row], axis=0)


def split(values, axis):
    high = values.astype(jnp.bfloat16)
    low = (values - high.astype(jnp.float32)).astype(jnp.bfloat16)
    return jnp.concatenate([high, low], axis=axis)


def from_right(values, table):
    count = values.shape[1]
    out = jnp.dot(split(values, 1), table, preferred_element_type=jnp.float32)
    return out[:, :count] + out[:, count:]


def from_left(table, values):
    count = table.shape[0] // 2
    out = jnp.dot(table, split(values, 0), preferred_element_type=jnp.float32)
    return out[:count] + out[count:]


def swap_blocks(parts, width):
    parts = list(parts)
    axis = parts[0].ndim - 1
    lanes = parts[0].shape[axis]
    block = lax.broadcasted_iota(jnp.int32, parts[0].shape, axis) // width
    half = len(parts) // 2
    while half:
        low_side = (block // half) % 2 == 0
        for first in range(len(parts)):
            if (first // half) % 2 == 0:
                one, two = parts[first], parts[first + half]
                parts[first] = jnp.where(low_side, one, pltpu.roll(two, half * width, axis))
                parts[first + half] = jnp.where(
                    low_side, pltpu.roll(one, lanes - half * width, axis), two
                )
        half //= 2
    return parts


def kernel(
    conc_hbm, mobility_hbm, kappa_hbm, well_depth_hbm, square_hbm, half_f_hbm, half_i_hbm, out,
    mobility, kappa, well_depth, conc, square_tables, half_f, half_i, own_mix,
    other, depths, other_depths, z_out, z_in, y_out, y_in, near, x_out, x_in, b_out, b_in, w_out, w_in,
    load, pair_sent, pair_got, sent, zr, yr, xr, br, wr,
):
    species, rows_x, rows_y, n = conc.shape
    me_sp, me_py, me_pz = lax.axis_index("sp"), lax.axis_index("py"), lax.axis_index("pz")
    count_pz = n // rows_y
    blocks = count_pz * PIECES
    units = species * PIECES
    last = units - 1
    width = n // blocks
    groups = rows_x // blocks
    sub = SUBLANES
    quarters = sub // 2
    mesh_id = pl.DeviceIdType.MESH

    half = me_py // 2
    inner = lax.rem(me_py + half, 2) == 1
    outer = jnp.logical_not(inner)
    buddy = {"sp": me_sp, "py": me_py + 1 - 2 * lax.rem(me_py, 2), "pz": me_pz}
    across = {"sp": me_sp, "py": 3 - me_py, "pz": me_pz}
    partner = {"sp": 1 - me_sp, "py": me_py, "pz": me_pz}
    others_pz = [3 - me_pz, me_pz + 1 - 2 * lax.rem(me_pz, 2), lax.rem(me_pz + 2, 4)]

    def along_pz(peer):
        return {"sp": me_sp, "py": me_py, "pz": peer}

    barrier = pltpu.get_barrier_semaphore()
    peers = [partner, buddy] + [along_pz(peer) for peer in others_pz]
    for peer in peers:
        pl.semaphore_signal(barrier, inc=1, device_id=peer, device_id_type=mesh_id)

    @pl.when(inner)
    def _():
        pl.semaphore_signal(barrier, inc=1, device_id=across, device_id_type=mesh_id)

    def lot(g):
        return pl.ds(g * blocks, blocks)

    moves = [(conc_hbm.at[:, lot(g)], conc.at[:, lot(g)]) for g in range(groups)]
    moves += [
        (well_depth_hbm, well_depth), (mobility_hbm, mobility), (kappa_hbm, kappa),
        (square_hbm, square_tables), (half_f_hbm.at[half], half_f), (half_i_hbm.at[half], half_i),
    ]
    loads = [
        pltpu.make_async_copy(source, target, load.at[i])
        for i, (source, target) in enumerate(moves)
    ]
    for copy in loads:
        copy.start()
    conc_loads, small_loads, table_loads = loads[:groups], loads[groups:-3], loads[-3:]
    right_f, left_f, left_i, right_i = (square_tables.at[i] for i in range(4))
    for copy in small_loads:
        copy.wait()
    for t in range(species):
        depths[t : t + 1, :] = jnp.full((1, n), well_depth[t], jnp.float32)
    pl.semaphore_wait(barrier, len(peers) + jnp.where(inner, 1, 0))

    def remote(source, target, send, recv, peer):
        return pltpu.make_async_remote_copy(
            src_ref=source, dst_ref=target, send_sem=send, recv_sem=recv,
            device_id=peer, device_id_type=mesh_id,
        )

    def waiter(lines, sem):
        return pltpu.make_async_remote_copy(
            src_ref=lines, dst_ref=lines, send_sem=sem, recv_sem=sem,
            device_id=partner, device_id_type=mesh_id,
        )

    depth_pair = remote(depths, other_depths, pair_sent.at[1], pair_got.at[groups], partner)
    pair = [
        remote(
            conc.at[:, lot(g)], other.at[:, lot(g)], pair_sent.at[0], pair_got.at[g], partner
        )
        for g in range(groups)
    ]
    for g in range(groups):
        conc_loads[g].wait()
        pair[g].start()
        if g == 0:
            depth_pair.start()

    y_rows = pl.ds(pl.multiple_of(me_pz * rows_y, rows_y), rows_y)
    z_sent, y_sent, x_sent, b_sent, w_sent = (sent.at[i] for i in range(5))

    def z_copy(chunk, peer, part):
        slot = chunk if chunk < 2 else chunk // 2 + 1
        return remote(
            z_out.at[chunk, peer, part], z_in.at[chunk, part, y_rows], z_sent,
            zr.at[slot], along_pz(peer),
        )

    def z_all(first, count, slot):
        lines = z_in.at[pl.ds(first, count), :, pl.ds(0, (count_pz - 1) * rows_y)]
        return waiter(lines, zr.at[slot])

    def rows_of(q):
        return pl.ds(pl.multiple_of(2 * rows_x * q, 2 * rows_x), 2 * rows_x)

    def slot_of(one):
        return lax.rem(one, SLOTS)

    def y_copy(one, f, q):
        chunk, rows = 2 * one + f, rows_of(q)
        return remote(
            y_out.at[chunk, rows], y_in.at[chunk, rows], y_sent, yr.at[slot_of(one), q], buddy
        )

    def y_all(one, q):
        return waiter(y_in.at[pl.ds(2 * one, 2), rows_of(q)], yr.at[slot_of(one), q])

    def x_copy(one, part, q):
        rows = rows_of(q)
        got = 2 * slot_of(one) + part
        if part:
            got = got + one // last * (2 * SLOTS + q - got)
        return remote(
            x_out.at[one, part, rows], x_in.at[one, part, rows], x_sent, xr.at[got], across
        )

    def x_all(one, part):
        return waiter(x_in.at[one, part], xr.at[2 * slot_of(one) + part])

    def b_all(one):
        return waiter(b_in.at[one], br.at[slot_of(one)])

    def w_copy(one, peer):
        return remote(
            w_out.at[one, peer], w_in.at[one, me_pz], w_sent, wr.at[one // PIECES], along_pz(peer)
        )

    def w_all(one):
        lines = w_in.at[pl.ds(PIECES * one, PIECES), pl.ds(0, count_pz - 1)]
        return waiter(lines, wr.at[one])

    def terms_of(one, side, field, depth):
        own_i = me_sp * species + one
        terms = []
        for t in range(species):
            j = side * species + t
            weight = mobility[own_i, j]
            terms.append((field, t, weight * depth[t : t + 1, :], weight * kappa[j]))
        return terms

    def mixed(terms, x, first=None, second=None):
        for field, t, bulk_weight, conc_weight in terms:
            c = field[t, x]
            a = bulk_weight * (c * c * c - c)
            b = conc_weight * c
            first = a if first is None else first + a
            second = b if second is None else second + b
        return first, second

    def z_part(one, g, opening=False):
        own = terms_of(one, me_sp, conc, depths)
        if opening and g == 0:
            for x in range(rows_x):
                own_mix[0, x], own_mix[1, x] = mixed(own, x)
            depth_pair.wait_recv()
        others = terms_of(one, 1 - me_sp, other, other_depths)
        if opening:
            pair[g].wait_recv()
        bulk_mix, conc_mix = [], []
        for block in range(blocks):
            x = g * blocks + block
            if opening:
                first, second = mixed(others, x, own_mix[0, x], own_mix[1, x])
            else:
                first, second = mixed(own + others, x)
            bulk_mix.append(first)
            conc_mix.append(second)
        modes = from_right(jnp.concatenate(bulk_mix + conc_mix, axis=0), right_f[...])
        modes = modes.reshape(2, blocks, rows_y, n)
        for f in range(2):
            swapped = swap_blocks([modes[f, block] for block in range(blocks)], width)
            for block in range(blocks):
                unit = PIECES * one + block % PIECES
                z_out[2 * unit + f, block // PIECES, g] = swapped[block]
        if opening:
            for c in range(2):
                for peer in others_pz:
                    z_copy(c, peer, pl.ds(g, 1)).start()
        if g == groups - 1:
            for c in range(2 if opening else 0, 2 * PIECES):
                for peer in others_pz:
                    z_copy(2 * PIECES * one + c, peer, pl.ds(0, groups)).start()
            for c in range(2 * PIECES):
                chunk = 2 * PIECES * one + c
                z_in[chunk, :, y_rows] = z_out[chunk, me_pz]

    def y_chunk(chunk):
        for g in range(0, groups, 2):
            lines = jnp.concatenate([z_in[chunk, g], z_in[chunk, g + 1]], axis=1)
            modes = from_left(left_f[...], lines)
            for h in range(2):
                part = modes[:, h * n : (h + 1) * n].reshape(blocks, sub, n)
                swapped = swap_blocks([part[b] for b in range(blocks)], width)
                for block in range(blocks):
                    x = (g + h) * blocks + block
                    y_out[chunk, pl.ds(x, sub, stride=rows_x), :] = swapped[block]

    def y_send(one):
        @pl.when(outer)
        def _():
            for q in range(quarters):
                for f in range(2):
                    y_copy(one, f, q).start()

    def square(index):
        freq = jnp.minimum(index, n - index).astype(jnp.float32)
        root = freq * (2.0 * math.pi / n)
        return root * root

    lane = lax.broadcasted_iota(jnp.int32, (1, n), 1)
    ksq_x = square(lax.broadcasted_iota(jnp.int32, (n, 1), 0))

    def x_quarter(one, q):
        y_all(one, q).wait_recv()
        own_i = me_sp * species + one // PIECES
        piece = me_pz * PIECES + lax.rem(one, PIECES)
        ksq_z = square(piece * width + lane % width)
        half_stiff = 0.5 * (mobility[own_i, own_i] * kappa[own_i])

        def line_rows(h):
            return pl.ds(pl.multiple_of((2 * q + h) * rows_x, rows_x), rows_x)

        both, ksq = [], []
        for f in range(2):
            chunk = 2 * one + f
            both.append(from_left(half_f[...], jnp.concatenate([
                jnp.concatenate([
                    field[chunk, line_rows(h), :] for field in (y_out, y_in)
                ], axis=0)
                for h in range(2)
            ], axis=1)))
        for h in range(2):
            ksq_y = square((lane // width) * sub + (2 * q + h))
            ksq.append(ksq_x + (ksq_y + ksq_z))
        ksq = jnp.concatenate(ksq, axis=1)
        drop = 0.5 * ksq * (both[0] + ksq * both[1]) / (1.0 + half_stiff * (ksq * ksq))
        lines = from_left(half_i[...], drop)
        for h in range(2):
            for i, (field, part) in enumerate([(near, 0), (near, 1), (x_out, 0), (x_out, 1)]):
                field[one, part, line_rows(h), :] = lines[
                    i * rows_x : (i + 1) * rows_x, h * n : (h + 1) * n
                ]
        x_copy(one, 1, q).start()
        x_copy(one, 0, q).start()

    def combine_outer(one):
        x_all(one, 1).wait_recv()
        b_out[one] = near[one, 1] + x_in[one, 1]
        remote(b_out.at[one], b_in.at[one], b_sent, br.at[slot_of(one)], buddy).start()

    def combine_inner(one):
        x_all(one, 0).wait_recv()
        b_in[one] = near[one, 0] + x_in[one, 0]

    def y_back(one):
        for g in range(0, groups, 2):
            pairs = []
            for h in range(2):
                parts = []
                for block in range(blocks):
                    x = (g + h) * blocks + block
                    parts.append(b_in[one, pl.ds(x, sub, stride=rows_x), :])
                swapped = swap_blocks(parts, width)
                pairs.append(jnp.stack(swapped, axis=0).reshape(n, n))
            lines = from_left(left_i[...], jnp.concatenate(pairs, axis=1))
            for h in range(2):
                part = lines[:, h * n : (h + 1) * n].reshape(count_pz, rows_y, n)
                w_out[one, :, g + h] = part
        for peer in others_pz:
            w_copy(one, peer).start()
        w_in[one, me_pz] = w_out[one, me_pz]

    def back(one):
        @pl.when(inner)
        def _():
            combine_inner(one)

        @pl.when(outer)
        def _():
            b_all(one).wait_recv()

        y_back(one)

    def z_back(one):
        w_all(one).wait_recv()
        for g in range(0, groups, 2):
            rows = []
            for h in range(2):
                rows += swap_blocks([
                    w_in[PIECES * one + block % PIECES, block // PIECES, g + h]
                    for block in range(blocks)
                ], width)
            lines = from_right(jnp.concatenate(rows, axis=0), right_i[...])
            lines = lines.reshape(2, blocks, rows_y, n)
            for h in range(2):
                for block in range(blocks):
                    x = (g + h) * blocks + block
                    out[one, x] = conc[one, x] - lines[h, block]

    table_loads[0].wait()
    for g in range(groups):
        z_part(0, g, True)
    for copy in table_loads[1:]:
        copy.wait()
    for g in range(groups):
        z_part(1, g)
    for f in range(2):
        z_all(f, 1, f).wait_recv()
        y_chunk(f)
    y_send(0)
    z_all(2, 2, 2).wait_recv()
    for f in range(2):
        y_chunk(2 + f)
    y_send(1)
    extra = {}
    for one in range(2, species):
        for g in range(groups):
            extra[1 + (one - 2) * groups + g] = functools.partial(z_part, one, g)
    for one in range(species - 1):
        extra[units - 2 * (species - 1 - one)] = functools.partial(z_back, one)

    def middle(step, _):
        one, q = step // quarters, lax.rem(step, quarters)
        ahead, behind = one + 2, one - 2

        @pl.when(inner)
        def _():
            x_quarter(one, q)

        @pl.when(jnp.logical_and(inner, jnp.logical_and(behind >= 0, q == 0)))
        def _():
            combine_outer(behind)

        @pl.when(jnp.logical_and(ahead < units, q == 0))
        def _():
            z_all(2 * ahead, 2, ahead + 1).wait_recv()

        @pl.when(jnp.logical_and(ahead < units, q < 2))
        def _():
            y_chunk(2 * ahead + q)

        @pl.when(jnp.logical_and(ahead < units, q == 1))
        def _():
            y_send(ahead)

        @pl.when(jnp.logical_and(behind >= 0, q == 2))
        def _():
            back(behind)

        for unit, work in extra.items():
            @pl.when(jnp.logical_and(one == unit, q == 3))
            def _(work=work):
                work()

        return 0

    lax.fori_loop(0, units * quarters, middle, 0)

    @pl.when(inner)
    def _():
        combine_outer(last - 1)

    back(last - 1)

    @pl.when(inner)
    def _():
        for q in range(quarters):
            rows = rows_of(q)
            x_copy(last, 1, q).wait_recv()
            b_out[last, rows, :] = near[last, 1, rows, :] + x_in[last, 1, rows, :]
            remote(
                b_out.at[last, rows], b_in.at[last, rows], b_sent, br.at[last % SLOTS], buddy
            ).start()
        combine_inner(last)

    @pl.when(outer)
    def _():
        b_all(last).wait_recv()

    y_back(last)
    z_back(species - 1)

    depth_pair.wait_send()
    waiter(conc, pair_sent.at[0]).wait_send()
    waiter(z_out.at[:, pl.ds(0, count_pz - 1)], z_sent).wait_send()

    @pl.when(outer)
    def _():
        waiter(y_out, y_sent).wait_send()

    @pl.when(inner)
    def _():
        waiter(x_out, x_sent).wait_send()
        waiter(b_out, b_sent).wait_send()

    waiter(w_out.at[:, pl.ds(0, count_pz - 1)], w_sent).wait_send()


def per_device_kernel(concentration, mobility, kappa, well_depth):
    species, rows_x, rows_y, n = concentration.shape
    count_py, count_pz = lax.axis_size("py"), lax.axis_size("pz")
    table = basis(n)
    forward = split_table(table)
    inverse = split_table(table.T)
    square_tables = np.stack([forward, forward.T, inverse.T, inverse])
    blocks = np.arange(n).reshape(count_py, rows_x)
    orders = [blocks[[1, 0, 2, 3]].reshape(n), blocks[[2, 3, 1, 0]].reshape(n)]
    half_forward = np.stack([split_table(table[order[: n // 2]]).T for order in orders])
    half_inverse = np.stack([split_table(table[order].T).T for order in orders])
    blocks = count_pz * PIECES
    units = species * PIECES
    groups = rows_x // blocks
    strip = rows_x * SUBLANES
    f32, bf16 = jnp.float32, jnp.bfloat16
    hbm = pl.BlockSpec(memory_space=pltpu.HBM)
    dma = pltpu.SemaphoreType.DMA

    def far(array):
        return pltpu.with_memory_space_constraint(array, pltpu.HBM)

    return pl.pallas_call(
        kernel,
        out_shape=jax.ShapeDtypeStruct(concentration.shape, f32),
        in_specs=[hbm] * 7,
        out_specs=pl.BlockSpec(memory_space=pltpu.VMEM),
        scratch_shapes=[
            pltpu.SMEM(mobility.shape, f32),
            pltpu.SMEM(kappa.shape, f32),
            pltpu.SMEM(well_depth.shape, f32),
            pltpu.VMEM((species, rows_x, rows_y, n), f32),
            pltpu.VMEM(square_tables.shape, bf16),
            pltpu.VMEM(half_forward.shape[1:], bf16),
            pltpu.VMEM(half_inverse.shape[1:], bf16),
            pltpu.VMEM((2, rows_x, rows_y, n), f32),
            pltpu.VMEM((species, rows_x, rows_y, n), f32),
            pltpu.VMEM((species, n), f32),
            pltpu.VMEM((species, n), f32),
            pltpu.VMEM((2 * units, count_pz, groups, rows_y, n), f32),
            pltpu.VMEM((2 * units, groups, n, n), f32),
            pltpu.VMEM((2 * units, strip, n), f32),
            pltpu.VMEM((2 * units, strip, n), f32),
            pltpu.VMEM((units, 2, strip, n), f32),
            pltpu.VMEM((units, 2, strip, n), f32),
            pltpu.VMEM((units, 2, strip, n), f32),
            pltpu.VMEM((units, strip, n), f32),
            pltpu.VMEM((units, strip, n), f32),
            pltpu.VMEM((units, count_pz, groups, rows_y, n), f32),
            pltpu.VMEM((units, count_pz, groups, rows_y, n), f32),
            dma((groups + 6,)), dma((2,)), dma((groups + 1,)), dma((5,)),
            dma((units + 1,)), dma((SLOTS, SUBLANES // 2)), dma((2 * SLOTS + 4,)), dma((SLOTS,)),
            dma((species,)),
        ],
        compiler_params=pltpu.CompilerParams(
            collective_id=0, has_side_effects=True, vmem_limit_bytes=46 * 1024 * 1024
        ),
        name="step",
    )(*(
        far(jnp.asarray(each)) for each in (
            concentration, mobility, kappa, well_depth, square_tables, half_forward, half_inverse
        )
    ))


def per_device(concentration, mobility, kappa, well_depth):
    species, rows_x, rows_y, n = concentration.shape
    count_sp, count_py, count_pz = (lax.axis_size(name) for name in ("sp", "py", "pz"))
    cube = rows_x * count_py == n and rows_y * count_pz == n and n == 128
    blocks = count_pz * PIECES
    whole = n == SUBLANES * blocks and rows_x % (2 * blocks) == 0 and rows_y % SUBLANES == 0
    if cube and whole and count_sp == 2 and count_py == 4 and count_pz == 4 and species == 4:
        return per_device_kernel(concentration, mobility, kappa, well_depth)
    return per_device_general(concentration, mobility, kappa, well_depth)


def solution(mesh):
    in_specs = (P("sp", "py", "pz", None), P(), P(), P("sp"))
    out_specs = P("sp", "py", "pz", None)
    return jax.shard_map(
        per_device, mesh=mesh, in_specs=in_specs, out_specs=out_specs, check_vma=False
    )
```

time: 125 us -> 120 us (0.960)
  Pallas kernels: 124 us -> 119 us
    pallas_call x1, Pallas kernels: 124 us -> 119 us  [per_device_kernel(): pl.pallas_call(kernel, out_shape=jax.ShapeDtypeStruct(concentration.shape...]
where the time goes in v2:
time: 120 us
  Pallas kernels  119 us (99%)
  local copies, waits for them, and re-layouts  1.32 us (1%)
    pallas_call x1, Pallas kernels, per_device_kernel(): pl.pallas_call(kernel, out_shape=jax.ShapeDtypeStruct(concentration.shape...  119 us

profile of v2, /device:TPU:0, one launch (start us, length us, event | category | flops | bytes accessed | tf_op | source)
XLA Modules:
  0.0 120.3 jit_solution(11015956561980092596)
XLA Ops:
  0.0 118.9 %step.1 = f32[4,32,32,128]{3,2,1,0:T(8,128)S(1)} custom-call(f32[4,32,32,128]{3,2,1,0:T(8,128)} %conc_hbm.1, f32[8,8]{1,0:T(8,128)} %mobility_hbm.1, f32[8]{0:T(128)} %kappa_hbm.1, f32[4]{0:T(128)} %well_depth_hbm.1, bf16[4,256,256]{2,1,0:T(8,128)(2,1)} %constant.6.clone.square_hbm, bf16[2,256,128]{2,1,0:T(8,128)(2,1)} %constant.7.clone.half_f_hbm, ...), custom_call_target="tpu_custom_call" | custom-call | tf_op jit(solution)/shard_map/step/pallas_call | solution.py:604
  119.0 1.3 %copy.9 = f32[4,32,32,128]{3,2,1,0:T(8,128)} copy(f32[4,32,32,128]{3,2,1,0:T(8,128)S(1)} %step.1) | data formatting | bytes 4194304

commit v3 on v2

--- a/solution.py
+++ b/solution.py
@@ -117,6 +117,9 @@
 PIECES = 4
 SUBLANES = 8
 SLOTS = 6
+STEPS = 16
+LAG = 5
+DIRECT = 2
 
 
 def basis(count):
@@ -196,7 +199,9 @@
     inner = lax.rem(me_py + half, 2) == 1
     outer = jnp.logical_not(inner)
     buddy = {"sp": me_sp, "py": me_py + 1 - 2 * lax.rem(me_py, 2), "pz": me_pz}
-    across = {"sp": me_sp, "py": 3 - me_py, "pz": me_pz}
+    across_py = 3 - me_py
+    far_py = lax.rem(me_py + 2, 4)
+    across = {"sp": me_sp, "py": across_py, "pz": me_pz}
     partner = {"sp": 1 - me_sp, "py": me_py, "pz": me_pz}
     others_pz = [3 - me_pz, me_pz + 1 - 2 * lax.rem(me_pz, 2), lax.rem(me_pz + 2, 4)]
 
@@ -290,15 +295,18 @@
 
     def x_copy(one, part, q):
         rows = rows_of(q)
-        got = 2 * slot_of(one) + part
+        got = slot_of(one)
+        target = across
         if part:
-            got = got + one // last * (2 * SLOTS + q - got)
+            got = SLOTS + lax.rem(one * quarters + q, STEPS)
+            direct = (one * quarters + q) // (units * quarters - DIRECT)
+            target = {"sp": me_sp, "py": across_py + direct * (far_py - across_py), "pz": me_pz}
         return remote(
-            x_out.at[one, part, rows], x_in.at[one, part, rows], x_sent, xr.at[got], across
-        )
-
-    def x_all(one, part):
-        return waiter(x_in.at[one, part], xr.at[2 * slot_of(one) + part])
+            x_out.at[one, part, rows], x_in.at[one, part, rows], x_sent, xr.at[got], target
+        )
+
+    def x_all(one):
+        return waiter(x_in.at[one, 0], xr.at[slot_of(one)])
 
     def b_all(one):
         return waiter(b_in.at[one], br.at[slot_of(one)])
@@ -426,13 +434,24 @@
         x_copy(one, 1, q).start()
         x_copy(one, 0, q).start()
 
-    def combine_outer(one):
-        x_all(one, 1).wait_recv()
-        b_out[one] = near[one, 1] + x_in[one, 1]
-        remote(b_out.at[one], b_in.at[one], b_sent, br.at[slot_of(one)], buddy).start()
+        @pl.when(one * quarters + q >= units * quarters - DIRECT)
+        def _():
+            rows = rows_of(q)
+            remote(
+                near.at[last, 1, rows], b_in.at[last, rows], b_sent, br.at[last % SLOTS], buddy
+            ).start()
+
+    def combine_quarter(step):
+        one, q = step // quarters, lax.rem(step, quarters)
+        rows = rows_of(q)
+        x_copy(one, 1, q).wait_recv()
+        b_out[one, rows, :] = near[one, 1, rows, :] + x_in[one, 1, rows, :]
+        remote(
+            b_out.at[one, rows], b_in.at[one, rows], b_sent, br.at[slot_of(one)], buddy
+        ).start()
 
     def combine_inner(one):
-        x_all(one, 0).wait_recv()
+        x_all(one).wait_recv()
         b_in[one] = near[one, 0] + x_in[one, 0]
 
     def y_back(one):
@@ -506,13 +525,13 @@
         one, q = step // quarters, lax.rem(step, quarters)
         ahead, behind = one + 2, one - 2
 
+        @pl.when(jnp.logical_and(inner, step >= LAG))
+        def _():
+            combine_quarter(step - LAG)
+
         @pl.when(inner)
         def _():
             x_quarter(one, q)
-
-        @pl.when(jnp.logical_and(inner, jnp.logical_and(behind >= 0, q == 0)))
-        def _():
-            combine_outer(behind)
 
         @pl.when(jnp.logical_and(ahead < units, q == 0))
         def _():
@@ -537,28 +556,31 @@
 
         return 0
 
-    lax.fori_loop(0, units * quarters, middle, 0)
+    steps = units * quarters
+    lax.fori_loop(0, steps, middle, 0)
+
+    def returns(step, _):
+        combine_quarter(step)
+        return 0
 
     @pl.when(inner)
     def _():
-        combine_outer(last - 1)
+        lax.fori_loop(steps - LAG, steps - quarters, returns, 0)
 
     back(last - 1)
 
     @pl.when(inner)
     def _():
-        for q in range(quarters):
-            rows = rows_of(q)
-            x_copy(last, 1, q).wait_recv()
-            b_out[last, rows, :] = near[last, 1, rows, :] + x_in[last, 1, rows, :]
-            remote(
-                b_out.at[last, rows], b_in.at[last, rows], b_sent, br.at[last % SLOTS], buddy
-            ).start()
+        lax.fori_loop(steps - quarters, steps - DIRECT, returns, 0)
         combine_inner(last)
 
     @pl.when(outer)
     def _():
         b_all(last).wait_recv()
+        for q in range(quarters - DIRECT, quarters):
+            x_copy(last, 1, q).wait_recv()
+            rows = rows_of(q)
+            b_in[last, rows, :] = b_in[last, rows, :] + x_in[last, 1, rows, :]
 
     y_back(last)
     z_back(species - 1)
@@ -630,7 +652,7 @@
             pltpu.VMEM((units, count_pz, groups, rows_y, n), f32),
             pltpu.VMEM((units, count_pz, groups, rows_y, n), f32),
             dma((groups + 6,)), dma((2,)), dma((groups + 1,)), dma((5,)),
-            dma((units + 1,)), dma((SLOTS, SUBLANES // 2)), dma((2 * SLOTS + 4,)), dma((SLOTS,)),
+            dma((units + 1,)), dma((SLOTS, SUBLANES // 2)), dma((SLOTS + STEPS,)), dma((SLOTS,)),
             dma((species,)),
         ],
         compiler_params=pltpu.CompilerParams(

time: 120 us -> 119 us (level)
  Pallas kernels: 119 us -> 117 us
    pallas_call x1, Pallas kernels: 119 us -> 117 us  [per_device_kernel(): pl.pallas_call(kernel, out_shape=jax.ShapeDtypeStruct(concentration.shape...]
where the time goes in v3:
time: 119 us
  Pallas kernels  117 us (98%)
  local copies, waits for them, and re-layouts  1.32 us (1%)
    pallas_call x1, Pallas kernels, per_device_kernel(): pl.pallas_call(kernel, out_shape=jax.ShapeDtypeStruct(concentration.shape...  117 us

profile of v3, /device:TPU:0, one launch (start us, length us, event | category | flops | bytes accessed | tf_op | source)
XLA Modules:
  0.0 118.8 jit_solution(8004104809929009346)
XLA Ops:
  0.0 117.4 %step.1 = f32[4,32,32,128]{3,2,1,0:T(8,128)S(1)} custom-call(f32[4,32,32,128]{3,2,1,0:T(8,128)} %conc_hbm.1, f32[8,8]{1,0:T(8,128)} %mobility_hbm.1, f32[8]{0:T(128)} %kappa_hbm.1, f32[4]{0:T(128)} %well_depth_hbm.1, bf16[4,256,256]{2,1,0:T(8,128)(2,1)} %constant.6.clone.square_hbm, bf16[2,256,128]{2,1,0:T(8,128)(2,1)} %constant.7.clone.half_f_hbm, ...), custom_call_target="tpu_custom_call" | custom-call | tf_op jit(solution)/shard_map/step/pallas_call | solution.py:626
  117.5 1.3 %copy.9 = f32[4,32,32,128]{3,2,1,0:T(8,128)} copy(f32[4,32,32,128]{3,2,1,0:T(8,128)S(1)} %step.1) | data formatting | bytes 4194304

commit v4 on v3

--- a/solution.py
+++ b/solution.py
@@ -116,10 +116,11 @@
 
 PIECES = 4
 SUBLANES = 8
-SLOTS = 6
-STEPS = 16
-LAG = 5
-DIRECT = 2
+SLOTS = 5
+STEPS = 10
+LAG = 4
+DIRECT = 3
+EARLY = 2
 
 
 def basis(count):
@@ -217,10 +218,16 @@
     def _():
         pl.semaphore_signal(barrier, inc=1, device_id=across, device_id_type=mesh_id)
 
-    def lot(g):
+    lots = 2 * groups
+    lot_rows = rows_x // lots
+
+    def lot(i):
+        return pl.ds(i * lot_rows, lot_rows)
+
+    def group(g):
         return pl.ds(g * blocks, blocks)
 
-    moves = [(conc_hbm.at[:, lot(g)], conc.at[:, lot(g)]) for g in range(groups)]
+    moves = [(conc_hbm.at[:, group(g)], conc.at[:, group(g)]) for g in range(groups)]
     moves += [
         (well_depth_hbm, well_depth), (mobility_hbm, mobility), (kappa_hbm, kappa),
         (square_hbm, square_tables), (half_f_hbm.at[half], half_f), (half_i_hbm.at[half], half_i),
@@ -251,24 +258,27 @@
             device_id=partner, device_id_type=mesh_id,
         )
 
-    depth_pair = remote(depths, other_depths, pair_sent.at[1], pair_got.at[groups], partner)
+    depth_pair = remote(depths, other_depths, pair_sent.at[1], pair_got.at[lots], partner)
     pair = [
         remote(
-            conc.at[:, lot(g)], other.at[:, lot(g)], pair_sent.at[0], pair_got.at[g], partner
+            conc.at[:, lot(i)], other.at[:, lot(i)], pair_sent.at[0], pair_got.at[i], partner
         )
-        for g in range(groups)
+        for i in range(lots)
     ]
     for g in range(groups):
         conc_loads[g].wait()
-        pair[g].start()
+        pair[2 * g].start()
         if g == 0:
             depth_pair.start()
+        pair[2 * g + 1].start()
 
     y_rows = pl.ds(pl.multiple_of(me_pz * rows_y, rows_y), rows_y)
     z_sent, y_sent, x_sent, b_sent, w_sent = (sent.at[i] for i in range(5))
 
     def z_copy(chunk, peer, part):
         slot = chunk if chunk < 2 else chunk // 2 + 1
+        if chunk >= 4 * PIECES:
+            slot = 2 * PIECES - 1 + chunk // (2 * PIECES)
         return remote(
             z_out.at[chunk, peer, part], z_in.at[chunk, part, y_rows], z_sent,
             zr.at[slot], along_pz(peer),
@@ -283,6 +293,9 @@
 
     def slot_of(one):
         return lax.rem(one, SLOTS)
+
+    def x_slot(one):
+        return lax.rem(one, SLOTS + 1)
 
     def y_copy(one, f, q):
         chunk, rows = 2 * one + f, rows_of(q)
@@ -295,10 +308,10 @@
 
     def x_copy(one, part, q):
         rows = rows_of(q)
-        got = slot_of(one)
+        got = x_slot(one)
         target = across
         if part:
-            got = SLOTS + lax.rem(one * quarters + q, STEPS)
+            got = SLOTS + 1 + lax.rem(one * quarters + q, STEPS)
             direct = (one * quarters + q) // (units * quarters - DIRECT)
             target = {"sp": me_sp, "py": across_py + direct * (far_py - across_py), "pz": me_pz}
         return remote(
@@ -306,19 +319,24 @@
         )
 
     def x_all(one):
-        return waiter(x_in.at[one, 0], xr.at[slot_of(one)])
+        return waiter(x_in.at[one, 0], xr.at[x_slot(one)])
 
     def b_all(one):
         return waiter(b_in.at[one], br.at[slot_of(one)])
 
-    def w_copy(one, peer):
+    def w_copy(one, peer, part, slot):
         return remote(
-            w_out.at[one, peer], w_in.at[one, me_pz], w_sent, wr.at[one // PIECES], along_pz(peer)
+            w_out.at[one, peer, part], w_in.at[one, me_pz, part], w_sent, wr.at[slot],
+            along_pz(peer),
         )
 
-    def w_all(one):
-        lines = w_in.at[pl.ds(PIECES * one, PIECES), pl.ds(0, count_pz - 1)]
+    def w_all(one, count):
+        lines = w_in.at[pl.ds(PIECES * one, count), pl.ds(0, count_pz - 1)]
         return waiter(lines, wr.at[one])
+
+    def w_last(g):
+        lines = w_in.at[last, pl.ds(0, count_pz - 1), pl.ds(g, 1)]
+        return waiter(lines, wr.at[species + g])
 
     def terms_of(one, side, field, depth):
         own_i = me_sp * species + one
@@ -345,28 +363,32 @@
                 own_mix[0, x], own_mix[1, x] = mixed(own, x)
             depth_pair.wait_recv()
         others = terms_of(one, 1 - me_sp, other, other_depths)
-        if opening:
-            pair[g].wait_recv()
-        bulk_mix, conc_mix = [], []
-        for block in range(blocks):
-            x = g * blocks + block
+        parts = 2 if opening else 1
+        modes = [[], []]
+        for i in range(parts):
             if opening:
-                first, second = mixed(others, x, own_mix[0, x], own_mix[1, x])
-            else:
-                first, second = mixed(own + others, x)
-            bulk_mix.append(first)
-            conc_mix.append(second)
-        modes = from_right(jnp.concatenate(bulk_mix + conc_mix, axis=0), right_f[...])
-        modes = modes.reshape(2, blocks, rows_y, n)
+                pair[2 * g + i].wait_recv()
+            bulk_mix, conc_mix = [], []
+            for block in range(i * blocks // parts, (i + 1) * blocks // parts):
+                x = g * blocks + block
+                if opening:
+                    first, second = mixed(others, x, own_mix[0, x], own_mix[1, x])
+                else:
+                    first, second = mixed(own + others, x)
+                bulk_mix.append(first)
+                conc_mix.append(second)
+            lines = from_right(jnp.concatenate(bulk_mix + conc_mix, axis=0), right_f[...])
+            lines = lines.reshape(2, blocks // parts, rows_y, n)
+            for f in range(2):
+                modes[f] += [lines[f, block] for block in range(blocks // parts)]
         for f in range(2):
-            swapped = swap_blocks([modes[f, block] for block in range(blocks)], width)
+            swapped = swap_blocks(modes[f], width)
             for block in range(blocks):
                 unit = PIECES * one + block % PIECES
                 z_out[2 * unit + f, block // PIECES, g] = swapped[block]
-        if opening:
-            for c in range(2):
+            if opening:
                 for peer in others_pz:
-                    z_copy(c, peer, pl.ds(g, 1)).start()
+                    z_copy(f, peer, pl.ds(g, 1)).start()
         if g == groups - 1:
             for c in range(2 if opening else 0, 2 * PIECES):
                 for peer in others_pz:
@@ -454,7 +476,7 @@
         x_all(one).wait_recv()
         b_in[one] = near[one, 0] + x_in[one, 0]
 
-    def y_back(one):
+    def y_back(one, closing=False):
         for g in range(0, groups, 2):
             pairs = []
             for h in range(2):
@@ -468,8 +490,13 @@
             for h in range(2):
                 part = lines[:, h * n : (h + 1) * n].reshape(count_pz, rows_y, n)
                 w_out[one, :, g + h] = part
-        for peer in others_pz:
-            w_copy(one, peer).start()
+        if closing:
+            for g in range(groups):
+                for peer in others_pz:
+                    w_copy(one, peer, pl.ds(g, 1), species + g).start()
+        else:
+            for peer in others_pz:
+                w_copy(one, peer, pl.ds(0, groups), one // PIECES).start()
         w_in[one, me_pz] = w_out[one, me_pz]
 
     def back(one):
@@ -483,21 +510,20 @@
 
         y_back(one)
 
-    def z_back(one):
-        w_all(one).wait_recv()
-        for g in range(0, groups, 2):
-            rows = []
-            for h in range(2):
-                rows += swap_blocks([
-                    w_in[PIECES * one + block % PIECES, block // PIECES, g + h]
-                    for block in range(blocks)
-                ], width)
+    def z_back(one, closing=False):
+        w_all(one, PIECES - 1 if closing else PIECES).wait_recv()
+        for g in range(groups):
+            if closing:
+                w_last(g).wait_recv()
+            rows = swap_blocks([
+                w_in[PIECES * one + block % PIECES, block // PIECES, g]
+                for block in range(blocks)
+            ], width)
             lines = from_right(jnp.concatenate(rows, axis=0), right_i[...])
-            lines = lines.reshape(2, blocks, rows_y, n)
-            for h in range(2):
-                for block in range(blocks):
-                    x = (g + h) * blocks + block
-                    out[one, x] = conc[one, x] - lines[h, block]
+            lines = lines.reshape(blocks, rows_y, n)
+            for block in range(blocks):
+                x = g * blocks + block
+                out[one, x] = conc[one, x] - lines[block]
 
     table_loads[0].wait()
     for g in range(groups):
@@ -509,7 +535,18 @@
     for f in range(2):
         z_all(f, 1, f).wait_recv()
         y_chunk(f)
-    y_send(0)
+
+        @pl.when(outer)
+        def _(f=f):
+            for q in range(EARLY):
+                y_copy(0, f, q).start()
+
+    @pl.when(outer)
+    def _():
+        for q in range(EARLY, quarters):
+            for f in range(2):
+                y_copy(0, f, q).start()
+
     z_all(2, 2, 2).wait_recv()
     for f in range(2):
         y_chunk(2 + f)
@@ -517,9 +554,9 @@
     extra = {}
     for one in range(2, species):
         for g in range(groups):
-            extra[1 + (one - 2) * groups + g] = functools.partial(z_part, one, g)
+            extra[2 + (one - 2) * groups + g] = functools.partial(z_part, one, g)
     for one in range(species - 1):
-        extra[units - 2 * (species - 1 - one)] = functools.partial(z_back, one)
+        extra[units + 1 - 2 * (species - 1 - one)] = functools.partial(z_back, one)
 
     def middle(step, _):
         one, q = step // quarters, lax.rem(step, quarters)
@@ -533,26 +570,31 @@
         def _():
             x_quarter(one, q)
 
-        @pl.when(jnp.logical_and(ahead < units, q == 0))
-        def _():
-            z_all(2 * ahead, 2, ahead + 1).wait_recv()
-
-        @pl.when(jnp.logical_and(ahead < units, q < 2))
-        def _():
-            y_chunk(2 * ahead + q)
-
-        @pl.when(jnp.logical_and(ahead < units, q == 1))
-        def _():
-            y_send(ahead)
-
-        @pl.when(jnp.logical_and(behind >= 0, q == 2))
-        def _():
-            back(behind)
-
         for unit, work in extra.items():
-            @pl.when(jnp.logical_and(one == unit, q == 3))
+            @pl.when(jnp.logical_and(one == unit, q == 0))
             def _(work=work):
                 work()
+
+        @pl.when(jnp.logical_and(ahead < 2 * PIECES, q == 1))
+        def _():
+            z_all(2 * ahead, 2, ahead + 1).wait_recv()
+
+        for each in range(2, species):
+            @pl.when(jnp.logical_and(ahead == PIECES * each, q == 1))
+            def _(each=each):
+                z_all(2 * PIECES * each, 2 * PIECES, 2 * PIECES - 1 + each).wait_recv()
+
+        @pl.when(jnp.logical_and(ahead < units, jnp.logical_and(q > 0, q < 3)))
+        def _():
+            y_chunk(2 * ahead + q - 1)
+
+        @pl.when(jnp.logical_and(ahead < units, q == 2))
+        def _():
+            y_send(ahead)
+
+        @pl.when(jnp.logical_and(behind >= 0, q == 3))
+        def _():
+            back(behind)
 
         return 0
 
@@ -582,8 +624,8 @@
             rows = rows_of(q)
             b_in[last, rows, :] = b_in[last, rows, :] + x_in[last, 1, rows, :]
 
-    y_back(last)
-    z_back(species - 1)
+    y_back(last, True)
+    z_back(species - 1, True)
 
     depth_pair.wait_send()
     waiter(conc, pair_sent.at[0]).wait_send()
@@ -651,9 +693,9 @@
             pltpu.VMEM((units, strip, n), f32),
             pltpu.VMEM((units, count_pz, groups, rows_y, n), f32),
             pltpu.VMEM((units, count_pz, groups, rows_y, n), f32),
-            dma((groups + 6,)), dma((2,)), dma((groups + 1,)), dma((5,)),
-            dma((units + 1,)), dma((SLOTS, SUBLANES // 2)), dma((SLOTS + STEPS,)), dma((SLOTS,)),
-            dma((species,)),
+            dma((groups + 6,)), dma((2,)), dma((2 * groups + 1,)), dma((5,)),
+            dma((2 * PIECES + species - 1,)), dma((SLOTS, SUBLANES // 2)), dma((SLOTS + 1 + STEPS,)), dma((SLOTS,)),
+            dma((species + groups,)),
         ],
         compiler_params=pltpu.CompilerParams(
             collective_id=0, has_side_effects=True, vmem_limit_bytes=46 * 1024 * 1024

time: 119 us -> 117 us (0.983)
    pallas_call x1, Pallas kernels: 117 us -> 116 us  [per_device_kernel(): pl.pallas_call(kernel, out_shape=jax.ShapeDtypeStruct(concentration.shape...]
where the time goes in v4:
time: 117 us
  Pallas kernels  116 us (99%)
  local copies, waits for them, and re-layouts  1.32 us (1%)
    pallas_call x1, Pallas kernels, per_device_kernel(): pl.pallas_call(kernel, out_shape=jax.ShapeDtypeStruct(concentration.shape...  116 us

profile of v4, /device:TPU:0, one launch (start us, length us, event | category | flops | bytes accessed | tf_op | source)
XLA Modules:
  0.0 117.0 jit_solution(55833678612815497)
XLA Ops:
  0.0 115.7 %step.1 = f32[4,32,32,128]{3,2,1,0:T(8,128)S(1)} custom-call(f32[4,32,32,128]{3,2,1,0:T(8,128)} %conc_hbm.1, f32[8,8]{1,0:T(8,128)} %mobility_hbm.1, f32[8]{0:T(128)} %kappa_hbm.1, f32[4]{0:T(128)} %well_depth_hbm.1, bf16[4,256,256]{2,1,0:T(8,128)(2,1)} %constant.6.clone.square_hbm, bf16[2,256,128]{2,1,0:T(8,128)(2,1)} %constant.7.clone.half_f_hbm, ...), custom_call_target="tpu_custom_call" | custom-call | tf_op jit(solution)/shard_map/step/pallas_call | solution.py:668
  115.7 1.3 %copy.9 = f32[4,32,32,128]{3,2,1,0:T(8,128)} copy(f32[4,32,32,128]{3,2,1,0:T(8,128)S(1)} %step.1) | data formatting | bytes 4194304

commit v5 on v4

--- a/solution.py
+++ b/solution.py
@@ -117,7 +117,7 @@
 PIECES = 4
 SUBLANES = 8
 SLOTS = 5
-STEPS = 10
+STEPS = 8
 LAG = 4
 DIRECT = 3
 EARLY = 2
@@ -512,9 +512,10 @@
 
     def z_back(one, closing=False):
         w_all(one, PIECES - 1 if closing else PIECES).wait_recv()
+        if closing:
+            for g in range(groups):
+                w_last(g).wait_recv()
         for g in range(groups):
-            if closing:
-                w_last(g).wait_recv()
             rows = swap_blocks([
                 w_in[PIECES * one + block % PIECES, block // PIECES, g]
                 for block in range(blocks)

time: 117 us -> 117 us (level)
  no operation moved by 1% of the time
where the time goes in v5:
time: 117 us
  Pallas kernels  116 us (99%)
  local copies, waits for them, and re-layouts  1.32 us (1%)
    pallas_call x1, Pallas kernels, per_device_kernel(): pl.pallas_call(kernel, out_shape=jax.ShapeDtypeStruct(concentration.shape...  116 us

profile of v5, /device:TPU:0, one launch (start us, length us, event | category | flops | bytes accessed | tf_op | source)
XLA Modules:
  0.0 117.0 jit_solution(16899791588587564706)
XLA Ops:
  0.0 115.7 %step.1 = f32[4,32,32,128]{3,2,1,0:T(8,128)S(1)} custom-call(f32[4,32,32,128]{3,2,1,0:T(8,128)} %conc_hbm.1, f32[8,8]{1,0:T(8,128)} %mobility_hbm.1, f32[8]{0:T(128)} %kappa_hbm.1, f32[4]{0:T(128)} %well_depth_hbm.1, bf16[4,256,256]{2,1,0:T(8,128)(2,1)} %constant.6.clone.square_hbm, bf16[2,256,128]{2,1,0:T(8,128)(2,1)} %constant.7.clone.half_f_hbm, ...), custom_call_target="tpu_custom_call" | custom-call | tf_op jit(solution)/shard_map/step/pallas_call | solution.py:669
  115.7 1.3 %copy.9 = f32[4,32,32,128]{3,2,1,0:T(8,128)} copy(f32[4,32,32,128]{3,2,1,0:T(8,128)S(1)} %step.1) | data formatting | bytes 4194304
